TPU v7x, 256 devices: a whole 4x4x8 slice. The times are simulated.
256 devices in a mesh: grp: 8 (over x, core), dp: 32 (over z, y).
Axes of the slice: x: 4, y: 4, z: 8, core: 2. Of those that a mesh axis runs over, the one named last changes fastest.
Arguments:
- gradients: bfloat16 [8, 32, 16384, 128], P('grp', 'dp'), may hold values from -48 to 48
- block_len: int32 [16], replicated, may hold values from 1 to 524288, 2097152 in all
- amax_history: float32 [4, 16], replicated, may hold values from 20 to 200
Outputs:
- mean_grad: bfloat16 [16384, 128], P('dp')
- block_amax: bfloat16 [16], replicated
Inputs may be any that keep to these rules, and one draw needn't show every extreme that they name: `block_len`: every tensor has at least one entry; the lengths sum to 2097152.
All inputs are finite; a program needn't handle non-finite values.
Results may differ from a plain program's by a relative error of at most 0.018.
Values may be sent and summed in bfloat16 or wider, within the bound.
No kernel may reach another device: no remote copies, remote signals or barrier semaphores. Data moves between devices by JAX's collectives and lax.ppermute only.
A program may use at most 64 MiB of HBM per device.

v0:
```python
import jax
import jax.numpy as jnp
from jax import lax
from jax.experimental import pallas as pl
from jax.experimental.pallas import tpu as pltpu
from jax.sharding import Mesh
from jax.sharding import PartitionSpec as P


SATURATE = 448.0
SIZE = {"x": 4, "c": 2, "z": 8, "y": 4}
ROWS = 512
A = 256
B = ROWS - A
BLOCKS = 16
DEVICES = 256


def shift(x, axis, by):
    n = SIZE[axis]
    return lax.ppermute(x, axis, [(i, (i + by) % n) for i in range(n)])


def f32(x):
    return x.astype(jnp.float32)


def add(*terms):
    total = f32(terms[0])
    for t in terms[1:]:
        total = total + f32(t)
    return total


def bf(x):
    return x.astype(jnp.bfloat16)


def together(*arrays):
    return lax.optimization_barrier(arrays)


def swap(x, axis, by):
    return lax.ppermute(x, axis, [(i, i ^ by) for i in range(SIZE[axis])])


def in_vmem(x):
    return pltpu.with_memory_space_constraint(x, pltpu.VMEM)


VMEM = pl.BlockSpec(memory_space=pltpu.VMEM)
SMEM = pl.BlockSpec(memory_space=pltpu.SMEM)


def prepare_kernel(at_ref, len_ref, hist_ref, block_ref, scale_ref):
    position = (
        (at_ref[0] * 4 + at_ref[1]) * (ROWS * 128)
        + lax.broadcasted_iota(jnp.int32, (ROWS, 128), 0) * 128
        + lax.broadcasted_iota(jnp.int32, (ROWS, 128), 1)
    )
    largest = jnp.maximum(jnp.max(hist_ref[...], axis=0, keepdims=True), 1.0)
    scales = SATURATE / largest
    block = jnp.zeros((ROWS, 128), jnp.int32)
    scale = jnp.broadcast_to(scales[:, 0:1], (ROWS, 128))
    end = jnp.int32(0)
    for c in range(1, BLOCKS):
        end = end + len_ref[c - 1]
        past = position >= end
        block = jnp.where(past, c, block)
        scale = jnp.where(past, scales[:, c : c + 1], scale)
    block_ref[...] = block
    scale_ref[...] = scale


def prepare(at, block_len, amax_history):
    return pl.pallas_call(
        prepare_kernel,
        out_shape=(
            jax.ShapeDtypeStruct((ROWS, 128), jnp.int32),
            jax.ShapeDtypeStruct((ROWS, 128), jnp.float32),
        ),
        in_specs=[SMEM, SMEM, VMEM],
        out_specs=[VMEM] * 2,
        name="prepare",
    )(at, block_len, amax_history)


def quantize_kernel(at_ref, block_ref, scale_ref, pa_ref, rows_ref, one_ref, two_ref, three_ref, pb_ref, up_ref, down_ref, far_ref, q_ref, m_ref, s_ref):
    z, y = at_ref[0], at_ref[1]
    s_ref[0:A] = add(pa_ref[z], rows_ref[0], one_ref[0], three_ref[0], two_ref[0])
    s_ref[A:ROWS] = add(pb_ref[y], up_ref[0], down_ref[0], far_ref[0])
    q_ref[...] = bf(jnp.clip(s_ref[...] * scale_ref[...], -SATURATE, SATURATE))
    size = jnp.abs(s_ref[...])
    block = block_ref[...]
    lane = lax.broadcasted_iota(jnp.int32, (8, 128), 1)
    tops = jnp.zeros((8, 128), jnp.float32)
    for c in range(BLOCKS):
        own = jnp.where(block == c, size, 0.0)
        own = jnp.max(own.reshape(ROWS // 8, 8, 128), axis=0)
        own = jnp.max(jnp.max(own, axis=0, keepdims=True), axis=1, keepdims=True)
        tops = jnp.where(lane == c, own, tops)
    m_ref[...] = jnp.broadcast_to(bf(tops[0:2])[None], (DEVICES, 2, 128))


def quantize(at, *arrays):
    return pl.pallas_call(
        quantize_kernel,
        out_shape=(
            jax.ShapeDtypeStruct((ROWS, 128), jnp.bfloat16),
            jax.ShapeDtypeStruct((DEVICES, 2, 128), jnp.bfloat16),
        ),
        in_specs=[SMEM] + [VMEM] * len(arrays),
        out_specs=[VMEM] * 2,
        scratch_shapes=[pltpu.VMEM((ROWS, 128), jnp.float32)],
        name="quantize",
    )(at, *[in_vmem(a) for a in arrays])


def head(whole, part):
    n = part.shape[0]
    return bf(add(whole, jnp.pad(part, ((0, n), (0, 0), (0, 0)))))


def tail(whole, part):
    n = part.shape[0]
    return bf(add(whole, jnp.pad(part, ((n, 0), (0, 0), (0, 0)))))


def send(x, axis, by, move=shift):
    return move(x, axis, by)


def both_ways(up, down, axis):
    return together(send(up, axis, 1), send(down, axis, -1))


def body(gradients, block_len, amax_history):
    g = gradients.reshape(8, 4, ROWS, 128)
    z, y = lax.axis_index("z"), lax.axis_index("y")

    def for_y(dy, z0=0, nz=8):
        at = (jnp.int32(z0), (y + dy) % 4, jnp.int32(0), jnp.int32(0))
        return lax.dynamic_slice(g, at, (nz, 1, A, 128)).reshape(nz, A, 128)

    def for_z(dz, y0=0, ny=4):
        at = ((z + dz) % 8, jnp.int32(y0), jnp.int32(A), jnp.int32(0))
        return lax.dynamic_slice(g, at, (1, ny, B, 128)).reshape(ny, B, 128)

    b_up, b_dn = both_ways(for_z(4, 0, 2), for_z(4, 2, 2), "z")
    a_up, a_dn = both_ways(for_y(2, 0, 4), for_y(2, 4, 4), "y")
    b_up, b_dn = both_ways(head(for_z(3), b_up), tail(for_z(-3), b_dn), "z")
    a_up, a_dn = both_ways(head(for_y(1), a_up), tail(for_y(-1), a_dn), "y")

    at = jnp.stack([z, y]).astype(jnp.int32)
    block, scale = prepare(at, block_len, amax_history)
    b_up, b_dn, block, scale = together(b_up, b_dn, block, scale)

    b_up, b_dn = both_ways(bf(add(for_z(2), b_up)), bf(add(for_z(-2), b_dn)), "z")
    b_up, b_dn = both_ways(bf(add(for_z(1), b_up)), bf(add(for_z(-1), b_dn)), "z")
    pa = bf(add(for_y(0), a_up, a_dn))

    def chunk(dz):
        return lax.dynamic_slice_in_dim(pa, (z + dz) % 8, 1, 0)

    a_up, a_dn = both_ways(
        jnp.concatenate([chunk(1), chunk(3)]), jnp.concatenate([chunk(-2), chunk(-4)]), "z"
    )
    pb = bf(add(for_z(0), b_up, b_dn))

    def piece(dy):
        return lax.dynamic_slice_in_dim(pb, (y + dy) % 4, 1, 0)

    b_far, b_up, b_dn = send(piece(2), "y", 2), send(piece(1), "y", 1), send(piece(-1), "y", -1)

    a_three = send(bf(add(chunk(-3), a_dn[1:2])), "z", -3)
    a_two = send(bf(add(chunk(2), a_up[1:2])), "z", 2)
    a_one = send(bf(add(chunk(-1), a_dn[0:1])), "z", -1)

    q, m = quantize(at, block, scale, pa, a_up, a_one, a_two, a_three, pb, b_up, b_dn, b_far)

    m = lax.all_to_all(m, ("x", "c", "z", "y"), split_axis=0, concat_axis=0, tiled=True)

    far, near, mirror = send(q, "x", 2, swap), send(q, "x", 1, swap), send(q, "x", 3, swap)
    chips = add(q, far) + add(near, mirror)
    accumulated = chips + send(chips, "c", 1)
    mean_grad = bf(accumulated / scale / DEVICES)
    return mean_grad, jnp.max(m, axis=(0, 1))[:BLOCKS]


def solution(mesh):
    torus = Mesh(mesh.devices.reshape(4, 2, 8, 4), ("x", "c", "z", "y"))
    placed = (P(("x", "c"), ("z", "y"), None, None), P(), P())
    return jax.shard_map(
        body, mesh=torus, in_specs=placed, out_specs=(P(("z", "y"), None), P()), check_vma=False
    )
```

profile of v0, /device:TPU:1, one launch (start us, length us, event | category | flops | bytes accessed | tf_op | source)
XLA Modules:
  0.0 97.3 jit_solution(14463333175567513986)
XLA Ops:
  1.6 2.5 %collective-permute-start = (bf16[2,256,128]{2,1,0:T(8,128)(2,1)S(1)}, bf16[2,256,128]{2,1,0:T(8,128)(2,1)S(1)}, u32[]{:S(2)}, u32[]{:S(2)}) collective-permute-start(bf16[2,256,128]{2,1,0:T(8,128)(2,1)S(1)} %get-tuple-element.57), channel_id=1, source_target_pairs={{0,4},{4,8},{8,12},{12,16},{16,20},{20,24},{24,28},{28,0},{1,5},{5... | collective-permute-start | bytes 393224 | tf_op jit(solution)/shard_map/ppermute | solution.py:21
  4.2 4.0 %collective-permute-start.1 = (bf16[2,256,128]{2,1,0:T(8,128)(2,1)S(1)}, bf16[2,256,128]{2,1,0:T(8,128)(2,1)S(1)}, u32[]{:S(2)}, u32[]{:S(2)}) collective-permute-start(bf16[2,256,128]{2,1,0:T(8,128)(2,1)S(1)} %get-tuple-element.56), channel_id=1, source_target_pairs={{0,28},{4,0},{8,4},{12,8},{16,12},{20,16},{24,20},{28,24},{1,29},{... | collective-permute-start | bytes 393224 | tf_op jit(solution)/shard_map/ppermute | solution.py:21
  9.3 1.4 %collective-permute-start.4 = (bf16[4,256,128]{2,1,0:T(8,128)(2,1)S(1)}, bf16[4,256,128]{2,1,0:T(8,128)(2,1)S(1)}, u32[]{:S(2)}, u32[]{:S(2)}) collective-permute-start(bf16[4,256,128]{2,1,0:T(8,128)(2,1)S(1)} %get-tuple-element.53), channel_id=1, source_target_pairs={{0,1},{1,2},{2,3},{3,0},{4,5},{5,6},{6,7},{7,4},{8,9},{9,10},{10,1... | collective-permute-start | bytes 786440 | tf_op jit(solution)/shard_map/ppermute | solution.py:21
  10.7 1.5 %collective-permute-start.5 = (bf16[4,256,128]{2,1,0:T(8,128)(2,1)S(1)}, bf16[4,256,128]{2,1,0:T(8,128)(2,1)S(1)}, u32[]{:S(2)}, u32[]{:S(2)}) collective-permute-start(bf16[4,256,128]{2,1,0:T(8,128)(2,1)S(1)} %get-tuple-element.52), channel_id=1, source_target_pairs={{0,3},{1,0},{2,1},{3,2},{4,7},{5,4},{6,5},{7,6},{8,11},{9,8},{10,9... | collective-permute-start | bytes 786440 | tf_op jit(solution)/shard_map/ppermute | solution.py:21
  12.2 1.8 %fusion.10 = (bf16[4,256,128]{2,1,0:T(8,128)(2,1)S(1)}, bf16[4,256,128]{2,1,0:T(8,128)(2,1)}) fusion(bf16[2,256,128]{2,1,0:T(8,128)(2,1)S(1)} %collective-permute-done.1, bf16[8,4,512,128]{3,2,1,0:T(8,128)(2,1)} %bitcast.48, s32[]{:T(128)S(6)} %select_n.132, bf16[2,256,128]{2,1,0:T(8,128)(2,1)S(1)} %collective-permute-done, s32[]{:T(128)S(6)} %select_n.128), kind=kLoop, calls=%fused_computation.19 | loop fusion | flops 1048576 | bytes 1310728 | tf_op jit(solution)/shard_map/convert_element_type | solution.py:36
  14.0 2.7 %collective-permute-start.3 = (bf16[4,256,128]{2,1,0:T(8,128)(2,1)S(1)}, bf16[4,256,128]{2,1,0:T(8,128)(2,1)S(1)}, u32[]{:S(2)}, u32[]{:S(2)}) collective-permute-start(bf16[4,256,128]{2,1,0:T(8,128)(2,1)S(1)} %get-tuple-element.54), channel_id=1, source_target_pairs={{0,28},{4,0},{8,4},{12,8},{16,12},{20,16},{24,20},{28,24},{1,29},{... | collective-permute-start | bytes 786440 | tf_op jit(solution)/shard_map/ppermute | solution.py:21
  17.6 1.4 %fusion = (bf16[8,256,128]{2,1,0:T(8,128)(2,1)S(1)}, bf16[8,256,128]{2,1,0:T(8,128)(2,1)S(1)}) fusion(bf16[4,256,128]{2,1,0:T(8,128)(2,1)S(1)} %collective-permute-done.5, bf16[8,4,512,128]{3,2,1,0:T(8,128)(2,1)} %bitcast.49, s32[]{:T(128)S(6)} %select_n.140, bf16[4,256,128]{2,1,0:T(8,128)(2,1)S(1)} %collective-permute-done.4, s32[]{:T(128)S(6)} %select_n.136), kind=kLoop, calls=%fused_computation.1 | loop fusion | flops 2097152 | bytes 2621448 | tf_op jit(solution)/shard_map/convert_element_type | solution.py:36
  20.0 1.7 %collective-permute-start.7 = (bf16[8,256,128]{2,1,0:T(8,128)(2,1)S(1)}, bf16[8,256,128]{2,1,0:T(8,128)(2,1)S(1)}, u32[]{:S(2)}, u32[]{:S(2)}) collective-permute-start(bf16[8,256,128]{2,1,0:T(8,128)(2,1)S(1)} %get-tuple-element.50), channel_id=1, source_target_pairs={{0,3},{1,0},{2,1},{3,2},{4,7},{5,4},{6,5},{7,6},{8,11},{9,8},{10,9... | collective-permute-start | bytes 1572872 | tf_op jit(solution)/shard_map/ppermute | solution.py:21
  22.4 2.1 %prepare.1 = (s32[512,128]{1,0:T(8,128)}, f32[512,128]{1,0:T(8,128)}) custom-call(s32[2]{0:T(128)} %pad_add_fusion.at_ref, s32[16]{0:T(128)} %len_ref.1, f32[4,16]{1,0:T(4,128)} %hist_ref.1), custom_call_target="tpu_custom_call" | custom-call | tf_op jit(solution)/shard_map/prepare/pallas_call | solution.py:76
  24.5 2.0 %fusion.5 = (bf16[4,256,128]{2,1,0:T(8,128)(2,1)}, bf16[4,256,128]{2,1,0:T(8,128)(2,1)}) fusion(bf16[4,256,128]{2,1,0:T(8,128)(2,1)S(1)} %collective-permute-done.3, bf16[8,4,512,128]{3,2,1,0:T(8,128)(2,1)} %bitcast.50, s32[]{:T(128)S(6)} %select_n.144, bf16[4,256,128]{2,1,0:T(8,128)(2,1)S(1)} %collective-permute-done.2, s32[]{:T(128)S(6)} %select_n.150), kind=kLoop, calls=%fused_computation.10 | loop fusion | flops 1048576 | bytes 1572872 | tf_op jit(solution)/shard_map/convert_element_type | solution.py:36
  26.6 2.7 %collective-permute-start.14 = (bf16[4,256,128]{2,1,0:T(8,128)(2,1)}, bf16[4,256,128]{2,1,0:T(8,128)(2,1)S(1)}, u32[]{:S(2)}, u32[]{:S(2)}) collective-permute-start(bf16[4,256,128]{2,1,0:T(8,128)(2,1)} %get-tuple-element.48), channel_id=1, source_target_pairs={{0,28},{4,0},{8,4},{12,8},{16,12},{20,16},{24,20},{28,24},{1,29},{... | collective-permute-start | bytes 786440 | tf_op jit(solution)/shard_map/ppermute | solution.py:21
  29.2 4.3 %collective-permute-done.13 = bf16[4,256,128]{2,1,0:T(8,128)(2,1)S(1)} collective-permute-done((bf16[4,256,128]{2,1,0:T(8,128)(2,1)}, bf16[4,256,128]{2,1,0:T(8,128)(2,1)S(1)}, u32[]{:S(2)}, u32[]{:S(2)}) %collective-permute-start.13) | collective-permute-done | bytes 262176 | tf_op jit(solution)/shard_map/ppermute | solution.py:21
  34.9 2.4 %collective-permute-start.9 = (bf16[2,256,128]{2,1,0:T(8,128)(2,1)S(1)}, bf16[2,256,128]{2,1,0:T(8,128)(2,1)S(1)}, u32[]{:S(2)}, u32[]{:S(2)}) collective-permute-start(bf16[2,256,128]{2,1,0:T(8,128)(2,1)S(1)} %pad_maximum_fusion.1), channel_id=1, source_target_pairs={{0,28},{4,0},{8,4},{12,8},{16,12},{20,16},{24,20},{28,24},{1,29},{... | collective-permute-start | bytes 393224 | tf_op jit(solution)/shard_map/ppermute | solution.py:21
  38.7 2.9 %collective-permute-start.16 = (bf16[4,256,128]{2,1,0:T(8,128)(2,1)S(1)}, bf16[4,256,128]{2,1,0:T(8,128)(2,1)S(1)}, u32[]{:S(2)}, u32[]{:S(2)}) collective-permute-start(bf16[4,256,128]{2,1,0:T(8,128)(2,1)S(1)} %get-tuple-element.46), channel_id=1, source_target_pairs={{0,28},{4,0},{8,4},{12,8},{16,12},{20,16},{24,20},{28,24},{1,29},{... | collective-permute-start | bytes 786440 | tf_op jit(solution)/shard_map/ppermute | solution.py:21
  43.1 3.4 %collective-permute-start.12 = (bf16[1,256,128]{2,1,0:T(8,128)(2,1)S(1)}, bf16[1,256,128]{2,1,0:T(8,128)(2,1)S(1)}, u32[]{:S(2)}, u32[]{:S(2)}) collective-permute-start(bf16[1,256,128]{2,1,0:T(8,128)(2,1)S(1)} %get-tuple-element.58), channel_id=1, source_target_pairs={{0,20},{4,24},{8,28},{12,0},{16,4},{20,8},{24,12},{28,16},{1,21},{... | collective-permute-start | bytes 196616 | tf_op jit(solution)/shard_map/ppermute | solution.py:21
  47.7 2.7 %collective-permute-start.18 = (bf16[1,256,128]{2,1,0:T(8,128)(2,1)S(1)}, bf16[1,256,128]{2,1,0:T(8,128)(2,1)S(1)}, u32[]{:S(2)}, u32[]{:S(2)}) collective-permute-start(bf16[1,256,128]{2,1,0:T(8,128)(2,1)S(1)} %get-tuple-element.66), channel_id=1, source_target_pairs={{0,3},{1,0},{2,1},{3,2},{4,7},{5,4},{6,5},{7,6},{8,11},{9,8},{10,9... | collective-permute-start | bytes 196616 | tf_op jit(solution)/shard_map/ppermute | solution.py:21
  50.4 1.6 %collective-permute-done.17.up_ref = bf16[1,256,128]{2,1,0:T(8,128)(2,1)S(1)} collective-permute-done((bf16[1,256,128]{2,1,0:T(8,128)(2,1)S(1)}, bf16[1,256,128]{2,1,0:T(8,128)(2,1)S(1)}, u32[]{:S(2)}, u32[]{:S(2)}) %collective-permute-start.17) | collective-permute-done | bytes 65568 | tf_op jit(solution)/shard_map/ppermute | solution.py:21
  52.0 3.1 %collective-permute-done.19.far_ref = bf16[1,256,128]{2,1,0:T(8,128)(2,1)S(1)} collective-permute-done((bf16[1,256,128]{2,1,0:T(8,128)(2,1)S(1)}, bf16[1,256,128]{2,1,0:T(8,128)(2,1)S(1)}, u32[]{:S(2)}, u32[]{:S(2)}) %collective-permute-start.19) | collective-permute-done | bytes 65568 | tf_op jit(solution)/shard_map/ppermute | solution.py:21
  55.1 2.0 %quantize.1 = (bf16[512,128]{1,0:T(8,128)(2,1)}, bf16[256,2,128]{2,1,0:T(2,128)(2,1)}) custom-call(s32[2]{0:T(128)} %pad_add_fusion.at_ref, s32[512,128]{1,0:T(8,128)S(1)} %copy-done.1, f32[512,128]{1,0:T(8,128)S(1)} %copy-done, bf16[8,256,128]{2,1,0:T(8,128)(2,1)S(1)} %fusion.3.pa_ref, bf16[2,256,128]{2,1,0:T(8,128)(2,1)S(1)} %collective-permute-done.8.rows_ref, ...), custom_call_target="tpu_custom_call" | custom-call | tf_op jit(solution)/shard_map/quantize/pallas_call | solution.py:106
  57.1 2.7 %collective-permute-start.20 = (bf16[512,128]{1,0:T(8,128)(2,1)}, bf16[512,128]{1,0:T(8,128)(2,1)S(1)}, u32[]{:S(2)}, u32[]{:S(2)}) collective-permute-start(bf16[512,128]{1,0:T(8,128)(2,1)} %get-tuple-element.44), channel_id=1, source_target_pairs={{0,128},{64,192},{128,0},{192,64},{1,129},{65,193},{129,1},{193,65... | collective-permute-start | bytes 393224 | tf_op jit(solution)/shard_map/ppermute | solution.py:44
  60.7 1.9 %collective-permute-done.20 = bf16[512,128]{1,0:T(8,128)(2,1)S(1)} collective-permute-done((bf16[512,128]{1,0:T(8,128)(2,1)}, bf16[512,128]{1,0:T(8,128)(2,1)S(1)}, u32[]{:S(2)}, u32[]{:S(2)}) %collective-permute-start.20) | collective-permute-done | bytes 131104 | tf_op jit(solution)/shard_map/ppermute | solution.py:44
  62.6 1.5 %collective-permute-done.21 = bf16[512,128]{1,0:T(8,128)(2,1)S(1)} collective-permute-done((bf16[512,128]{1,0:T(8,128)(2,1)}, bf16[512,128]{1,0:T(8,128)(2,1)S(1)}, u32[]{:S(2)}, u32[]{:S(2)}) %collective-permute-start.21) | collective-permute-done | bytes 131104 | tf_op jit(solution)/shard_map/ppermute | solution.py:44
  66.4 9.4 %collective-permute-start.23 = (f32[512,128]{1,0:T(8,128)S(1)}, f32[512,128]{1,0:T(8,128)S(1)}, u32[]{:S(2)}, u32[]{:S(2)}) collective-permute-start(f32[512,128]{1,0:T(8,128)S(1)} %add_add_fusion), channel_id=1, source_target_pairs={{0,32},{32,0},{1,33},{33,1},{2,34},{34,2},{3,35},{35,3},{4,36},{36... | collective-permute-start | bytes 786440 | tf_op jit(solution)/shard_map/ppermute | solution.py:21
  75.8 20.0 %all_to_all.5 = bf16[256,2,128]{2,1,0:T(2,128)(2,1)S(1)} all-to-all(bf16[256,2,128]{2,1,0:T(2,128)(2,1)} %get-tuple-element.45), channel_id=1, replica_groups=mesh['x'=4,'c'=2,'z'=8,'y'=4] {'x','c','z','y'}, dimensions={0} | all-to-all | bytes 262144 | tf_op jit(solution)/shard_map/all_to_all | solution.py:181
  (48 shorter events, 14.7 us)
Async XLA Ops:
  1.6 10.5 %collective-permute-start = (bf16[2,256,128]{2,1,0:T(8,128)(2,1)S(1)}, bf16[2,256,128]{2,1,0:T(8,128)(2,1)S(1)}, u32[]{:S(2)}, u32[]{:S(2)}) collective-permute-start(bf16[2,256,128]{2,1,0:T(8,128)(2,1)S(1)} %get-tuple-element.57), channel_id=1, source_target_pairs={{0,4},{4,8},{8,12},{12,16},{16,20},{20,24},{24,28},{28,0},{1,5},{5... | collective-permute-start | bytes 393224 | tf_op jit(solution)/shard_map/ppermute | solution.py:21
  4.2 8.0 %collective-permute-start.1 = (bf16[2,256,128]{2,1,0:T(8,128)(2,1)S(1)}, bf16[2,256,128]{2,1,0:T(8,128)(2,1)S(1)}, u32[]{:S(2)}, u32[]{:S(2)}) collective-permute-start(bf16[2,256,128]{2,1,0:T(8,128)(2,1)S(1)} %get-tuple-element.56), channel_id=1, source_target_pairs={{0,28},{4,0},{8,4},{12,8},{16,12},{20,16},{24,20},{28,24},{1,29},{... | collective-permute-start | bytes 393224 | tf_op jit(solution)/shard_map/ppermute | solution.py:21
  9.3 8.3 %collective-permute-start.4 = (bf16[4,256,128]{2,1,0:T(8,128)(2,1)S(1)}, bf16[4,256,128]{2,1,0:T(8,128)(2,1)S(1)}, u32[]{:S(2)}, u32[]{:S(2)}) collective-permute-start(bf16[4,256,128]{2,1,0:T(8,128)(2,1)S(1)} %get-tuple-element.53), channel_id=1, source_target_pairs={{0,1},{1,2},{2,3},{3,0},{4,5},{5,6},{6,7},{7,4},{8,9},{9,10},{10,1... | collective-permute-start | bytes 786440 | tf_op jit(solution)/shard_map/ppermute | solution.py:21
  10.7 7.0 %collective-permute-start.5 = (bf16[4,256,128]{2,1,0:T(8,128)(2,1)S(1)}, bf16[4,256,128]{2,1,0:T(8,128)(2,1)S(1)}, u32[]{:S(2)}, u32[]{:S(2)}) collective-permute-start(bf16[4,256,128]{2,1,0:T(8,128)(2,1)S(1)} %get-tuple-element.52), channel_id=1, source_target_pairs={{0,3},{1,0},{2,1},{3,2},{4,7},{5,4},{6,5},{7,6},{8,11},{9,8},{10,9... | collective-permute-start | bytes 786440 | tf_op jit(solution)/shard_map/ppermute | solution.py:21
  14.0 10.5 %collective-permute-start.2 = (bf16[4,256,128]{2,1,0:T(8,128)(2,1)}, bf16[4,256,128]{2,1,0:T(8,128)(2,1)S(1)}, u32[]{:S(2)}, u32[]{:S(2)}) collective-permute-start(bf16[4,256,128]{2,1,0:T(8,128)(2,1)} %get-tuple-element.55), channel_id=1, source_target_pairs={{0,4},{4,8},{8,12},{12,16},{16,20},{20,24},{24,28},{28,0},{1,5},{5... | collective-permute-start | bytes 786440 | tf_op jit(solution)/shard_map/ppermute | solution.py:21
  14.0 10.5 %collective-permute-start.3 = (bf16[4,256,128]{2,1,0:T(8,128)(2,1)S(1)}, bf16[4,256,128]{2,1,0:T(8,128)(2,1)S(1)}, u32[]{:S(2)}, u32[]{:S(2)}) collective-permute-start(bf16[4,256,128]{2,1,0:T(8,128)(2,1)S(1)} %get-tuple-element.54), channel_id=1, source_target_pairs={{0,28},{4,0},{8,4},{12,8},{16,12},{20,16},{24,20},{28,24},{1,29},{... | collective-permute-start | bytes 786440 | tf_op jit(solution)/shard_map/ppermute | solution.py:21
  19.0 14.6 %collective-permute-start.6 = (bf16[8,256,128]{2,1,0:T(8,128)(2,1)S(1)}, bf16[8,256,128]{2,1,0:T(8,128)(2,1)S(1)}, u32[]{:S(2)}, u32[]{:S(2)}) collective-permute-start(bf16[8,256,128]{2,1,0:T(8,128)(2,1)S(1)} %get-tuple-element.51), channel_id=1, source_target_pairs={{0,1},{1,2},{2,3},{3,0},{4,5},{5,6},{6,7},{7,4},{8,9},{9,10},{10,1... | collective-permute-start | bytes 1572872 | tf_op jit(solution)/shard_map/ppermute | solution.py:21
  20.0 13.5 %collective-permute-start.7 = (bf16[8,256,128]{2,1,0:T(8,128)(2,1)S(1)}, bf16[8,256,128]{2,1,0:T(8,128)(2,1)S(1)}, u32[]{:S(2)}, u32[]{:S(2)}) collective-permute-start(bf16[8,256,128]{2,1,0:T(8,128)(2,1)S(1)} %get-tuple-element.50), channel_id=1, source_target_pairs={{0,3},{1,0},{2,1},{3,2},{4,7},{5,4},{6,5},{7,6},{8,11},{9,8},{10,9... | collective-permute-start | bytes 1572872 | tf_op jit(solution)/shard_map/ppermute | solution.py:21
  26.6 7.0 %collective-permute-start.13 = (bf16[4,256,128]{2,1,0:T(8,128)(2,1)}, bf16[4,256,128]{2,1,0:T(8,128)(2,1)S(1)}, u32[]{:S(2)}, u32[]{:S(2)}) collective-permute-start(bf16[4,256,128]{2,1,0:T(8,128)(2,1)} %get-tuple-element.49), channel_id=1, source_target_pairs={{0,4},{4,8},{8,12},{12,16},{16,20},{20,24},{24,28},{28,0},{1,5},{5... | collective-permute-start | bytes 786440 | tf_op jit(solution)/shard_map/ppermute | solution.py:21
  26.6 7.0 %collective-permute-start.14 = (bf16[4,256,128]{2,1,0:T(8,128)(2,1)}, bf16[4,256,128]{2,1,0:T(8,128)(2,1)S(1)}, u32[]{:S(2)}, u32[]{:S(2)}) collective-permute-start(bf16[4,256,128]{2,1,0:T(8,128)(2,1)} %get-tuple-element.48), channel_id=1, source_target_pairs={{0,28},{4,0},{8,4},{12,8},{16,12},{20,16},{24,20},{28,24},{1,29},{... | collective-permute-start | bytes 786440 | tf_op jit(solution)/shard_map/ppermute | solution.py:21
  34.9 6.7 %collective-permute-start.9 = (bf16[2,256,128]{2,1,0:T(8,128)(2,1)S(1)}, bf16[2,256,128]{2,1,0:T(8,128)(2,1)S(1)}, u32[]{:S(2)}, u32[]{:S(2)}) collective-permute-start(bf16[2,256,128]{2,1,0:T(8,128)(2,1)S(1)} %pad_maximum_fusion.1), channel_id=1, source_target_pairs={{0,28},{4,0},{8,4},{12,8},{16,12},{20,16},{24,20},{28,24},{1,29},{... | collective-permute-start | bytes 393224 | tf_op jit(solution)/shard_map/ppermute | solution.py:21
  37.3 5.1 %collective-permute-start.8 = (bf16[2,256,128]{2,1,0:T(8,128)(2,1)S(1)}, bf16[2,256,128]{2,1,0:T(8,128)(2,1)S(1)}, u32[]{:S(2)}, u32[]{:S(2)}) collective-permute-start(bf16[2,256,128]{2,1,0:T(8,128)(2,1)S(1)} %pad_maximum_fusion), channel_id=1, source_target_pairs={{0,4},{4,8},{8,12},{12,16},{16,20},{20,24},{24,28},{28,0},{1,5},{5... | collective-permute-start | bytes 393224 | tf_op jit(solution)/shard_map/ppermute | solution.py:21
  38.6 7.9 %collective-permute-start.15 = (bf16[4,256,128]{2,1,0:T(8,128)(2,1)S(1)}, bf16[4,256,128]{2,1,0:T(8,128)(2,1)S(1)}, u32[]{:S(2)}, u32[]{:S(2)}) collective-permute-start(bf16[4,256,128]{2,1,0:T(8,128)(2,1)S(1)} %get-tuple-element.47), channel_id=1, source_target_pairs={{0,4},{4,8},{8,12},{12,16},{16,20},{20,24},{24,28},{28,0},{1,5},{5... | collective-permute-start | bytes 786440 | tf_op jit(solution)/shard_map/ppermute | solution.py:21
  38.7 7.8 %collective-permute-start.16 = (bf16[4,256,128]{2,1,0:T(8,128)(2,1)S(1)}, bf16[4,256,128]{2,1,0:T(8,128)(2,1)S(1)}, u32[]{:S(2)}, u32[]{:S(2)}) collective-permute-start(bf16[4,256,128]{2,1,0:T(8,128)(2,1)S(1)} %get-tuple-element.46), channel_id=1, source_target_pairs={{0,28},{4,0},{8,4},{12,8},{16,12},{20,16},{24,20},{28,24},{1,29},{... | collective-permute-start | bytes 786440 | tf_op jit(solution)/shard_map/ppermute | solution.py:21
  42.5 7.9 %collective-permute-start.10 = (bf16[1,256,128]{2,1,0:T(8,128)(2,1)S(1)}, bf16[1,256,128]{2,1,0:T(8,128)(2,1)S(1)}, u32[]{:S(2)}, u32[]{:S(2)}) collective-permute-start(bf16[1,256,128]{2,1,0:T(8,128)(2,1)S(1)} %get-tuple-element.59), channel_id=1, source_target_pairs={{0,28},{4,0},{8,4},{12,8},{16,12},{20,16},{24,20},{28,24},{1,29},{... | collective-permute-start | bytes 196616 | tf_op jit(solution)/shard_map/ppermute | solution.py:21
  42.9 7.4 %collective-permute-start.11 = (bf16[1,256,128]{2,1,0:T(8,128)(2,1)S(1)}, bf16[1,256,128]{2,1,0:T(8,128)(2,1)S(1)}, u32[]{:S(2)}, u32[]{:S(2)}) collective-permute-start(bf16[1,256,128]{2,1,0:T(8,128)(2,1)S(1)} %get-tuple-element.60), channel_id=1, source_target_pairs={{0,8},{4,12},{8,16},{12,20},{16,24},{20,28},{24,0},{28,4},{1,9},{5... | collective-permute-start | bytes 196616 | tf_op jit(solution)/shard_map/ppermute | solution.py:21
  43.1 7.2 %collective-permute-start.12 = (bf16[1,256,128]{2,1,0:T(8,128)(2,1)S(1)}, bf16[1,256,128]{2,1,0:T(8,128)(2,1)S(1)}, u32[]{:S(2)}, u32[]{:S(2)}) collective-permute-start(bf16[1,256,128]{2,1,0:T(8,128)(2,1)S(1)} %get-tuple-element.58), channel_id=1, source_target_pairs={{0,20},{4,24},{8,28},{12,0},{16,4},{20,8},{24,12},{28,16},{1,21},{... | collective-permute-start | bytes 196616 | tf_op jit(solution)/shard_map/ppermute | solution.py:21
  47.6 4.4 %collective-permute-start.17 = (bf16[1,256,128]{2,1,0:T(8,128)(2,1)S(1)}, bf16[1,256,128]{2,1,0:T(8,128)(2,1)S(1)}, u32[]{:S(2)}, u32[]{:S(2)}) collective-permute-start(bf16[1,256,128]{2,1,0:T(8,128)(2,1)S(1)} %get-tuple-element.67), channel_id=1, source_target_pairs={{0,1},{1,2},{2,3},{3,0},{4,5},{5,6},{6,7},{7,4},{8,9},{9,10},{10,1... | collective-permute-start | bytes 196616 | tf_op jit(solution)/shard_map/ppermute | solution.py:21
  47.7 4.3 %collective-permute-start.18 = (bf16[1,256,128]{2,1,0:T(8,128)(2,1)S(1)}, bf16[1,256,128]{2,1,0:T(8,128)(2,1)S(1)}, u32[]{:S(2)}, u32[]{:S(2)}) collective-permute-start(bf16[1,256,128]{2,1,0:T(8,128)(2,1)S(1)} %get-tuple-element.66), channel_id=1, source_target_pairs={{0,3},{1,0},{2,1},{3,2},{4,7},{5,4},{6,5},{7,6},{8,11},{9,8},{10,9... | collective-permute-start | bytes 196616 | tf_op jit(solution)/shard_map/ppermute | solution.py:21
  50.3 4.7 %collective-permute-start.19 = (bf16[1,256,128]{2,1,0:T(8,128)(2,1)S(1)}, bf16[1,256,128]{2,1,0:T(8,128)(2,1)S(1)}, u32[]{:S(2)}, u32[]{:S(2)}) collective-permute-start(bf16[1,256,128]{2,1,0:T(8,128)(2,1)S(1)} %get-tuple-element.65), channel_id=1, source_target_pairs={{0,2},{1,3},{2,0},{3,1},{4,6},{5,7},{6,4},{7,5},{8,10},{9,11},{10,... | collective-permute-start | bytes 196616 | tf_op jit(solution)/shard_map/ppermute | solution.py:21
  57.1 5.5 %collective-permute-start.20 = (bf16[512,128]{1,0:T(8,128)(2,1)}, bf16[512,128]{1,0:T(8,128)(2,1)S(1)}, u32[]{:S(2)}, u32[]{:S(2)}) collective-permute-start(bf16[512,128]{1,0:T(8,128)(2,1)} %get-tuple-element.44), channel_id=1, source_target_pairs={{0,128},{64,192},{128,0},{192,64},{1,129},{65,193},{129,1},{193,65... | collective-permute-start | bytes 393224 | tf_op jit(solution)/shard_map/ppermute | solution.py:44
  59.8 4.3 %collective-permute-start.21 = (bf16[512,128]{1,0:T(8,128)(2,1)}, bf16[512,128]{1,0:T(8,128)(2,1)S(1)}, u32[]{:S(2)}, u32[]{:S(2)}) collective-permute-start(bf16[512,128]{1,0:T(8,128)(2,1)} %get-tuple-element.44), channel_id=1, source_target_pairs={{0,64},{64,0},{128,192},{192,128},{1,65},{65,1},{129,193},{193,129... | collective-permute-start | bytes 393224 | tf_op jit(solution)/shard_map/ppermute | solution.py:44
  60.1 5.2 %collective-permute-start.22 = (bf16[512,128]{1,0:T(8,128)(2,1)}, bf16[512,128]{1,0:T(8,128)(2,1)S(1)}, u32[]{:S(2)}, u32[]{:S(2)}) collective-permute-start(bf16[512,128]{1,0:T(8,128)(2,1)} %get-tuple-element.44), channel_id=1, source_target_pairs={{0,192},{64,128},{128,64},{192,0},{1,193},{65,129},{129,65},{193,1... | collective-permute-start | bytes 393224 | tf_op jit(solution)/shard_map/ppermute | solution.py:44
  66.4 30.3 %collective-permute-start.23 = (f32[512,128]{1,0:T(8,128)S(1)}, f32[512,128]{1,0:T(8,128)S(1)}, u32[]{:S(2)}, u32[]{:S(2)}) collective-permute-start(f32[512,128]{1,0:T(8,128)S(1)} %add_add_fusion), channel_id=1, source_target_pairs={{0,32},{32,0},{1,33},{33,1},{2,34},{34,2},{3,35},{35,3},{4,36},{36... | collective-permute-start | bytes 786440 | tf_op jit(solution)/shard_map/ppermute | solution.py:21
  (2 other events, 61.1 us)
where the time goes:
time: 97.7 us; the launch traced here: 97.3 us
  starting transfers between devices  42.9 us (44%)
  blocking collectives  20 us (20%)
  waiting for transfers between devices  15.5 us (16%)
  other arithmetic  11.9 us (12%)
  Pallas kernels  4.16 us (4%)
  local copies, waits for them, and re-layouts  2.12 us (2%)
    ppermute x21, starting transfers between devices, shift(): return lax.ppermute(x, axis, [(i, (i + by) % n) for i in range(n)])  39.3 us
    all_to_all x1, blocking collectives, body(): lax.all_to_all(m, ('x', 'c', 'z', 'y'), split_axis=0, concat_axis=0, tile...  20 us
    ppermute x21, waiting for transfers between devices, shift(): return lax.ppermute(x, axis, [(i, (i + by) % n) for i in range(n)])  10.8 us
    convert_element_type x8, other arithmetic, bf(): return x.astype(jnp.bfloat16)  9.45 us
    ppermute x3, waiting for transfers between devices, swap(): return lax.ppermute(x, axis, [(i, i ^ by) for i in range(SIZE[axis])])  4.69 us
    ppermute x3, starting transfers between devices, swap(): return lax.ppermute(x, axis, [(i, i ^ by) for i in range(SIZE[axis])])  3.61 us
    pallas_call x1, Pallas kernels, prepare(): pl.pallas_call(prepare_kernel, out_shape=(jax.ShapeDtypeStruct((ROWS, 128...  2.14 us
    pallas_call x1, Pallas kernels, quantize(): pl.pallas_call(quantize_kernel, out_shape=(jax.ShapeDtypeStruct((ROWS, 12...  2.02 us
  transfers between devices with their start and end apart: 24, of which 8 were waited for; matrix products, arithmetic and copies ran while one was open for 10% of the time, Pallas kernels for 2%

commit v1 on v0

v1 whole, which is shorter than its diff:
```python
import functools

import jax
import jax.numpy as jnp
from jax import lax
from jax.experimental import pallas as pl
from jax.experimental.pallas import tpu as pltpu
from jax.sharding import Mesh
from jax.sharding import PartitionSpec as P


SATURATE = 448.0
SIZE = {"x": 4, "c": 2, "z": 8, "y": 4}
ROWS = 512
A = 288
B = ROWS - A
BLOCKS = 16
DEVICES = 256


def shift(x, axis, by):
    n = SIZE[axis]
    return lax.ppermute(x, axis, [(i, (i + by) % n) for i in range(n)])


def f32(x):
    return x.astype(jnp.float32)


def add(*terms):
    total = f32(terms[0])
    for t in terms[1:]:
        total = total + f32(t)
    return total


def bf(x):
    return x.astype(jnp.bfloat16)


def together(*arrays):
    return lax.optimization_barrier(arrays)


def swap(x, axis, by):
    return lax.ppermute(x, axis, [(i, i ^ by) for i in range(SIZE[axis])])


def in_vmem(x):
    return pltpu.with_memory_space_constraint(x, pltpu.VMEM)


VMEM = pl.BlockSpec(memory_space=pltpu.VMEM)
SMEM = pl.BlockSpec(memory_space=pltpu.SMEM)
SMALL = pltpu.CompilerParams(vmem_limit_bytes=8 << 20)


def prepare_kernel(at_ref, len_ref, hist_ref, block_ref, scale_ref):
    position = (
        (at_ref[0] * 4 + at_ref[1]) * (ROWS * 128)
        + lax.broadcasted_iota(jnp.int32, (ROWS, 128), 0) * 128
        + lax.broadcasted_iota(jnp.int32, (ROWS, 128), 1)
    )
    largest = jnp.maximum(jnp.max(hist_ref[...], axis=0, keepdims=True), 1.0)
    scales = SATURATE / largest
    block = jnp.zeros((ROWS, 128), jnp.int32)
    scale = jnp.broadcast_to(scales[:, 0:1], (ROWS, 128))
    end = jnp.int32(0)
    for c in range(1, BLOCKS):
        end = end + len_ref[c - 1]
        past = position >= end
        block = jnp.where(past, c, block)
        scale = jnp.where(past, scales[:, c : c + 1], scale)
    block_ref[...] = block
    scale_ref[...] = scale


def prepare(at, block_len, amax_history):
    return pl.pallas_call(
        prepare_kernel,
        out_shape=(
            jax.ShapeDtypeStruct((ROWS, 128), jnp.int32),
            jax.ShapeDtypeStruct((ROWS, 128), jnp.float32),
        ),
        in_specs=[SMEM, SMEM, VMEM],
        out_specs=[VMEM] * 2,
        name="prepare",
        compiler_params=SMALL,
    )(at, block_len, amax_history)


def call(kernel, out, at, *arrays, scratch=()):
    made = pl.pallas_call(
        kernel,
        out_shape=[pltpu.VMEM(shape, jnp.bfloat16) for shape in out],
        in_specs=[SMEM] + [SMEM if a.ndim == 1 else VMEM for a in arrays],
        out_specs=[VMEM] * len(out),
        scratch_shapes=scratch,
        compiler_params=SMALL,
    )(at, *[a if a.ndim == 1 else in_vmem(a) for a in arrays])
    return made


def copied(body, out, at, g):
    return pl.pallas_call(
        body,
        out_shape=[pltpu.VMEM(shape, jnp.bfloat16) for shape in out],
        in_specs=[SMEM, pl.BlockSpec(memory_space=pltpu.HBM)],
        out_specs=[VMEM] * len(out),
        scratch_shapes=[pltpu.SemaphoreType.DMA((8,))],
        compiler_params=SMALL,
    )(at, pltpu.with_memory_space_constraint(g, pltpu.HBM))


def run_copies(sems, pairs):
    copies = [pltpu.make_async_copy(src, dst, sems.at[i]) for i, (src, dst) in enumerate(pairs)]
    for copy in copies:
        copy.start()
    for copy in copies:
        copy.wait()


def open_kernel(at_ref, g_ref, far_z_ref, up_ref, down_ref, sems):
    z, y = at_ref[0], at_ref[1]
    row = (y + 2) % 4
    run_copies(sems, [
        (g_ref.at[(z + 4) % 8, :, A:], far_z_ref),
        (g_ref.at[0:4, row, :A], up_ref),
        (g_ref.at[4:8, row, :A], down_ref),
    ])


def stage_kernel(at_ref, g_ref, out_ref, sems):
    run_copies(sems, [(g_ref.at[i], out_ref.at[i]) for i in range(8)])


def b_first_kernel(at_ref, g_ref, got_ref, up_ref, down_ref):
    z = at_ref[0]
    odd = (z % 2).astype(jnp.float32)
    got = f32(got_ref[...])
    up_ref[...] = bf(f32(g_ref[(z + 3) % 8, :, A:]) + got * odd)
    down_ref[...] = bf(f32(g_ref[(z + 5) % 8, :, A:]) + got * (1.0 - odd))


def b_next_kernel(by, at_ref, g_ref, got_up_ref, got_down_ref, up_ref, down_ref):
    z = at_ref[0]
    up_ref[...] = bf(add(g_ref[(z + by) % 8, :, A:], got_up_ref[...]))
    down_ref[...] = bf(add(g_ref[(z + 8 - by) % 8, :, A:], got_down_ref[...]))


def b_last_kernel(at_ref, g_ref, got_up_ref, got_down_ref, keep_ref, give_ref):
    z, y = at_ref[0], at_ref[1]
    other = y + 1 - 2 * (y % 2)
    for ref, slot, row in ((keep_ref, 0, y), (keep_ref, 1, 3 - y), (give_ref, 0, other), (give_ref, 1, 3 - other)):
        ref[slot] = bf(add(g_ref[z, row, A:], got_up_ref[row], got_down_ref[row]))


def a_first_kernel(at_ref, g_ref, got_up_ref, got_down_ref, up_ref, down_ref):
    y = at_ref[1]
    up, down = (y + 1) % 4, (y + 3) % 4
    up_ref[0:4] = bf(add(g_ref[0:4, up, :A], got_up_ref[...]))
    up_ref[4:8] = g_ref[4:8, up, :A]
    down_ref[0:4] = g_ref[0:4, down, :A]
    down_ref[4:8] = bf(add(g_ref[4:8, down, :A], got_down_ref[...]))


def a_last_kernel(at_ref, g_ref, got_up_ref, got_down_ref, own_ref, up_ref, down_ref, near_ref):
    z, y = at_ref[0], at_ref[1]
    wanted = ((up_ref, 0, 1), (up_ref, 1, 3), (down_ref, 0, 6), (down_ref, 1, 4))
    wanted += ((near_ref, 0, 7), (near_ref, 1, 5), (near_ref, 2, 2), (own_ref, 0, 0))
    for ref, slot, by in wanted:
        row = (z + by) % 8
        ref[slot] = bf(add(g_ref[row, y, :A], got_up_ref[row], got_down_ref[row]))


def quantize_kernel(at_ref, len_ref, block_ref, scale_ref, pa_ref, rows_ref, one_ref, two_ref, three_ref, pb_ref, half_ref, last_ref, q_ref, m_ref, s_ref):
    s_ref[0:A] = add(pa_ref[0], rows_ref[0], one_ref[0], three_ref[0], two_ref[0])
    s_ref[A:ROWS] = add(pb_ref[0], half_ref[0], last_ref[0])
    q_ref[...] = bf(jnp.clip(s_ref[...] * scale_ref[...], -SATURATE, SATURATE))
    start = (at_ref[0] * 4 + at_ref[1]) * (ROWS * 128)
    low, high, end = jnp.int32(0), jnp.int32(0), jnp.int32(0)
    for c in range(BLOCKS - 1):
        end = end + len_ref[c]
        low = low + (start >= end).astype(jnp.int32)
        high = high + (start + (ROWS * 128 - 1) >= end).astype(jnp.int32)
    lane = lax.broadcasted_iota(jnp.int32, (8, 128), 1)

    def one_tensor(c, tops):
        own = jnp.where(block_ref[...] == c, jnp.abs(s_ref[...]), 0.0)
        own = jnp.max(own.reshape(ROWS // 8, 8, 128), axis=0)
        own = jnp.max(jnp.max(own, axis=0, keepdims=True), axis=1, keepdims=True)
        return jnp.where(lane == c, own, tops)

    tops = lax.fori_loop(low, high + 1, one_tensor, jnp.zeros((8, 128), jnp.float32))
    m_ref[...] = jnp.broadcast_to(bf(tops[0:2])[None], m_ref.shape)


def exchange(x, axes):
    return lax.all_to_all(x, axes, split_axis=0, concat_axis=0, tiled=True)


def send(x, axis, by, move=shift):
    return move(x, axis, by)


def both_ways(up, down, axis):
    return send(up, axis, 1), send(down, axis, -1)


def body(gradients, block_len, amax_history):
    g = gradients.reshape(8, 4, ROWS, 128)
    z, y = lax.axis_index("z"), lax.axis_index("y")
    at = jnp.stack([z, y]).astype(jnp.int32)

    four_z, eight_z, four_y = (4, B, 128), (8, A, 128), (2, A, 128)
    got, a_up, a_dn = copied(open_kernel, (four_z, (4, A, 128), (4, A, 128)), at, g)
    got = send(got, "z", 1, swap)
    a_up, a_dn = both_ways(a_up, a_dn, "y")
    (g,) = copied(stage_kernel, ((8, 4, ROWS, 128),), at, g)
    b_up, b_dn = call(b_first_kernel, (four_z, four_z), at, g, got)
    b_up, b_dn = both_ways(b_up, b_dn, "z")
    a_up, a_dn = call(a_first_kernel, (eight_z, eight_z), at, g, a_up, a_dn)
    a_up, a_dn = both_ways(a_up, a_dn, "y")

    block, scale = prepare(at, block_len, amax_history)
    b_up, b_dn, block, scale = together(b_up, b_dn, block, scale)

    b_up, b_dn = call(functools.partial(b_next_kernel, 2), (four_z, four_z), at, g, b_up, b_dn)
    b_up, b_dn = both_ways(b_up, b_dn, "z")
    b_up, b_dn = call(functools.partial(b_next_kernel, 1), (four_z, four_z), at, g, b_up, b_dn)
    b_up, b_dn = both_ways(b_up, b_dn, "z")

    pa, a_up, a_dn, near = call(a_last_kernel, ((1, A, 128), four_y, four_y, (3, A, 128)), at, g, a_up, a_dn)
    a_up, a_dn = both_ways(a_up, a_dn, "z")
    half = (2, B, 128)
    pb, half = call(b_last_kernel, (half, half), at, g, b_up, b_dn)
    half = send(half, "y", 1, swap)

    a_three = send(bf(add(near[1:2], a_dn[1:2])), "z", -3)
    a_two = send(bf(add(near[2:3], a_up[1:2])), "z", 2)
    a_one = send(bf(add(near[0:1], a_dn[0:1])), "z", -1)

    last = send(bf(add(pb[1:2], half[1:2])), "y", 3, swap)

    q, m = call(
        quantize_kernel, ((ROWS, 128), (DEVICES // 2, 2, 128)),
        at, block_len, block, scale, pa, a_up, a_one, a_two, a_three, pb, half, last,
        scratch=[pltpu.VMEM((ROWS, 128), jnp.float32)],
    )

    m = exchange(m, ("x", "z", "y"))

    far, near, mirror = send(q, "x", 2, swap), send(q, "x", 1, swap), send(q, "x", 3, swap)
    chips = add(q, far) + add(near, mirror)
    accumulated = chips + send(chips, "c", 1)
    mean_grad = bf(accumulated / scale / DEVICES)
    m, mean_grad = together(m, mean_grad)
    m = jnp.max(m, axis=0)
    m = jnp.maximum(m, send(m, "c", 1))
    return mean_grad, jnp.max(m, axis=0)[:BLOCKS]


def solution(mesh):
    torus = Mesh(mesh.devices.reshape(4, 2, 8, 4), ("x", "c", "z", "y"))
    placed = (P(("x", "c"), ("z", "y"), None, None), P(), P())
    return jax.shard_map(
        body, mesh=torus, in_specs=placed, out_specs=(P(("z", "y"), None), P()), check_vma=False
    )
```

time: 97.7 us -> 98.2 us (level)
  blocking collectives: 20 us -> 0 us
  starting transfers between devices: 42.9 us -> 56.2 us
  waiting for transfers between devices: 15.5 us -> 28.1 us
  other arithmetic: 11.9 us -> 1.61 us
  Pallas kernels: 4.16 us -> 11.3 us
  local copies, waits for them, and re-layouts: 2.12 us -> 0.01 us
    all_to_all x1 -> x0, blocking collectives: 20 us -> none  [body(): lax.all_to_all(m, ('x', 'c', 'z', 'y'), split_axis=0, concat_axis=0, tile...]
    all_to_all x0 -> x1, starting transfers between devices: none -> 11.6 us  [exchange(): return lax.all_to_all(x, axes, split_axis=0, concat_axis=0, tiled=True)]
    all_to_all x0 -> x1, waiting for transfers between devices: none -> 9.88 us  [exchange(): return lax.all_to_all(x, axes, split_axis=0, concat_axis=0, tiled=True)]
    convert_element_type x8 -> x3, other arithmetic: 9.45 us -> 0.8 us  [bf(): return x.astype(jnp.bfloat16)]
    pallas_call x1 -> x9, Pallas kernels: 2.02 us -> 10.1 us  [the longest x7 5.55 us: call(): pl.pallas_call(kernel, out_shape=[pltpu.VMEM(shape, jnp.bfloat16) for sha...]
    ppermute x3 -> x6, starting transfers between devices: 3.61 us -> 7.38 us  [swap(): return lax.ppermute(x, axis, [(i, i ^ by) for i in range(SIZE[axis])])]
    reshape x2 -> x0, local copies, waits for them, and re-layouts: 2.06 us -> none  [the longest x1 1.06 us: for_y(): return lax.dynamic_slice(g, at, (nz, 1, A, 128)).reshape(nz, A, 128)]
    ppermute x21 -> x17, starting transfers between devices: 39.3 us -> 37.3 us  [shift(): return lax.ppermute(x, axis, [(i, (i + by) % n) for i in range(n)])]
  transfers between devices with their start and end apart: 24 -> 24, of which waited for: 8 -> 13; matrix products, arithmetic and copies ran while one was open for 10% -> 1% of each run, Pallas kernels for 2% -> 8%
where the time goes in v1:
time: 98.2 us; the launch traced here: 98.1 us
  starting transfers between devices  56.2 us (57%)
  waiting for transfers between devices  28.1 us (29%)
  Pallas kernels  11.3 us (12%)
  other arithmetic  1.61 us (2%)
    ppermute x17, starting transfers between devices, shift(): return lax.ppermute(x, axis, [(i, (i + by) % n) for i in range(n)])  37.3 us
    ppermute x17, waiting for transfers between devices, shift(): return lax.ppermute(x, axis, [(i, (i + by) % n) for i in range(n)])  11.8 us
    all_to_all x1, starting transfers between devices, exchange(): return lax.all_to_all(x, axes, split_axis=0, concat_axis=0, tiled=True)  11.6 us
    all_to_all x1, waiting for transfers between devices, exchange(): return lax.all_to_all(x, axes, split_axis=0, concat_axis=0, tiled=True)  9.88 us
    ppermute x6, starting transfers between devices, swap(): return lax.ppermute(x, axis, [(i, i ^ by) for i in range(SIZE[axis])])  7.38 us
    ppermute x6, waiting for transfers between devices, swap(): return lax.ppermute(x, axis, [(i, i ^ by) for i in range(SIZE[axis])])  6.48 us
    pallas_call x7, Pallas kernels, call(): pl.pallas_call(kernel, out_shape=[pltpu.VMEM(shape, jnp.bfloat16) for sha...  5.55 us
    pallas_call x2, Pallas kernels, copied(): pl.pallas_call(body, out_shape=[pltpu.VMEM(shape, jnp.bfloat16) for shape...  4.55 us
  transfers between devices with their start and end apart: 24, of which 13 were waited for; matrix products, arithmetic and copies ran while one was open for 1% of the time, Pallas kernels for 8%

profile of v1, /device:TPU:1, one launch (start us, length us, event | category | flops | bytes accessed | tf_op | source)
XLA Modules:
  0.0 98.1 jit_solution(10333599036254083213)
XLA Ops:
  0.7 1.8 %shard_map.51 = (bf16[4,224,128]{2,1,0:T(8,128)(2,1)S(1)}, bf16[4,288,128]{2,1,0:T(8,128)(2,1)S(1)}, bf16[4,288,128]{2,1,0:T(8,128)(2,1)S(1)}) custom-call(s32[2]{0:T(128)S(1)} %pad_add_fusion.at_ref, bf16[8,4,512,128]{3,2,1,0:T(8,128)(2,1)} %bitcast.4), custom_call_target="tpu_custom_call" | custom-call | tf_op jit(solution)/shard_map/pallas_call | solution.py:105
  2.5 2.2 %collective-permute-start.3 = (bf16[4,288,128]{2,1,0:T(8,128)(2,1)S(1)}, bf16[4,288,128]{2,1,0:T(8,128)(2,1)S(1)}, u32[]{:S(2)}, u32[]{:S(2)}) collective-permute-start(bf16[4,288,128]{2,1,0:T(8,128)(2,1)S(1)} %get-tuple-element.36), channel_id=1, source_target_pairs={{0,1},{1,2},{2,3},{3,0},{4,5},{5,6},{6,7},{7,4},{8,9},{9,10},{10,1... | collective-permute-start | bytes 884744 | tf_op jit(solution)/shard_map/ppermute | solution.py:23
  4.7 1.5 %collective-permute-start.4 = (bf16[4,288,128]{2,1,0:T(8,128)(2,1)S(1)}, bf16[4,288,128]{2,1,0:T(8,128)(2,1)S(1)}, u32[]{:S(2)}, u32[]{:S(2)}) collective-permute-start(bf16[4,288,128]{2,1,0:T(8,128)(2,1)S(1)} %get-tuple-element.37), channel_id=1, source_target_pairs={{0,3},{1,0},{2,1},{3,2},{4,7},{5,4},{6,5},{7,6},{8,11},{9,8},{10,9... | collective-permute-start | bytes 884744 | tf_op jit(solution)/shard_map/ppermute | solution.py:23
  6.2 1.6 %collective-permute-start = (bf16[4,224,128]{2,1,0:T(8,128)(2,1)S(1)}, bf16[4,224,128]{2,1,0:T(8,128)(2,1)S(1)}, u32[]{:S(2)}, u32[]{:S(2)}) collective-permute-start(bf16[4,224,128]{2,1,0:T(8,128)(2,1)S(1)} %get-tuple-element.29), channel_id=1, source_target_pairs={{0,4},{4,0},{8,12},{12,8},{16,20},{20,16},{24,28},{28,24},{1,5},{5... | collective-permute-start | bytes 688136 | tf_op jit(solution)/shard_map/ppermute | solution.py:46
  7.9 2.8 %shard_map.50.g_ref = bf16[8,4,512,128]{3,2,1,0:T(8,128)(2,1)S(1)} custom-call(s32[2]{0:T(128)S(1)} %pad_add_fusion.at_ref, bf16[8,4,512,128]{3,2,1,0:T(8,128)(2,1)} %bitcast.5), custom_call_target="tpu_custom_call" | custom-call | tf_op jit(solution)/shard_map/pallas_call | solution.py:105
  12.8 1.6 %collective-permute-start.5 = (bf16[8,288,128]{2,1,0:T(8,128)(2,1)S(1)}, bf16[8,288,128]{2,1,0:T(8,128)(2,1)S(1)}, u32[]{:S(2)}, u32[]{:S(2)}) collective-permute-start(bf16[8,288,128]{2,1,0:T(8,128)(2,1)S(1)} %get-tuple-element.38), channel_id=1, source_target_pairs={{0,1},{1,2},{2,3},{3,0},{4,5},{5,6},{6,7},{7,4},{8,9},{9,10},{10,1... | collective-permute-start | bytes 1769480 | tf_op jit(solution)/shard_map/ppermute | solution.py:23
  16.2 2.3 %collective-permute-start.1 = (bf16[4,224,128]{2,1,0:T(8,128)(2,1)S(1)}, bf16[4,224,128]{2,1,0:T(8,128)(2,1)S(1)}, u32[]{:S(2)}, u32[]{:S(2)}) collective-permute-start(bf16[4,224,128]{2,1,0:T(8,128)(2,1)S(1)} %get-tuple-element.30), channel_id=1, source_target_pairs={{0,4},{4,8},{8,12},{12,16},{16,20},{20,24},{24,28},{28,0},{1,5},{5... | collective-permute-start | bytes 688136 | tf_op jit(solution)/shard_map/ppermute | solution.py:23
  18.5 4.0 %collective-permute-start.2 = (bf16[4,224,128]{2,1,0:T(8,128)(2,1)S(1)}, bf16[4,224,128]{2,1,0:T(8,128)(2,1)S(1)}, u32[]{:S(2)}, u32[]{:S(2)}) collective-permute-start(bf16[4,224,128]{2,1,0:T(8,128)(2,1)S(1)} %get-tuple-element.31), channel_id=1, source_target_pairs={{0,28},{4,0},{8,4},{12,8},{16,12},{20,16},{24,20},{28,24},{1,29},{... | collective-permute-start | bytes 688136 | tf_op jit(solution)/shard_map/ppermute | solution.py:23
  23.7 2.6 %collective-permute-done.1.got_up_ref = bf16[4,224,128]{2,1,0:T(8,128)(2,1)S(1)} collective-permute-done((bf16[4,224,128]{2,1,0:T(8,128)(2,1)S(1)}, bf16[4,224,128]{2,1,0:T(8,128)(2,1)S(1)}, u32[]{:S(2)}, u32[]{:S(2)}) %collective-permute-start.1) | collective-permute-done | bytes 229408 | tf_op jit(solution)/shard_map/ppermute | solution.py:23
  27.1 2.7 %collective-permute-start.13 = (bf16[4,224,128]{2,1,0:T(8,128)(2,1)S(1)}, bf16[4,224,128]{2,1,0:T(8,128)(2,1)S(1)}, u32[]{:S(2)}, u32[]{:S(2)}) collective-permute-start(bf16[4,224,128]{2,1,0:T(8,128)(2,1)S(1)} %get-tuple-element.47), channel_id=1, source_target_pairs={{0,28},{4,0},{8,4},{12,8},{16,12},{20,16},{24,20},{28,24},{1,29},{... | collective-permute-start | bytes 688136 | tf_op jit(solution)/shard_map/ppermute | solution.py:23
  29.8 3.4 %collective-permute-done.12.got_up_ref = bf16[4,224,128]{2,1,0:T(8,128)(2,1)S(1)} collective-permute-done((bf16[4,224,128]{2,1,0:T(8,128)(2,1)S(1)}, bf16[4,224,128]{2,1,0:T(8,128)(2,1)S(1)}, u32[]{:S(2)}, u32[]{:S(2)}) %collective-permute-start.12) | collective-permute-done | bytes 229408 | tf_op jit(solution)/shard_map/ppermute | solution.py:23
  33.9 2.0 %collective-permute-start.14 = (bf16[4,224,128]{2,1,0:T(8,128)(2,1)S(1)}, bf16[4,224,128]{2,1,0:T(8,128)(2,1)S(1)}, u32[]{:S(2)}, u32[]{:S(2)}) collective-permute-start(bf16[4,224,128]{2,1,0:T(8,128)(2,1)S(1)} %get-tuple-element.48), channel_id=1, source_target_pairs={{0,4},{4,8},{8,12},{12,16},{16,20},{20,24},{24,28},{28,0},{1,5},{5... | collective-permute-start | bytes 688136 | tf_op jit(solution)/shard_map/ppermute | solution.py:23
  38.5 1.7 %collective-permute-start.8 = (bf16[2,288,128]{2,1,0:T(8,128)(2,1)S(1)}, bf16[2,288,128]{2,1,0:T(8,128)(2,1)S(1)}, u32[]{:S(2)}, u32[]{:S(2)}) collective-permute-start(bf16[2,288,128]{2,1,0:T(8,128)(2,1)S(1)} %get-tuple-element.43), channel_id=1, source_target_pairs={{0,28},{4,0},{8,4},{12,8},{16,12},{20,16},{24,20},{28,24},{1,29},{... | collective-permute-start | bytes 442376 | tf_op jit(solution)/shard_map/ppermute | solution.py:23
  41.8 2.2 %collective-permute-done.7.rows_ref = bf16[2,288,128]{2,1,0:T(8,128)(2,1)S(1)} collective-permute-done((bf16[2,288,128]{2,1,0:T(8,128)(2,1)S(1)}, bf16[2,288,128]{2,1,0:T(8,128)(2,1)S(1)}, u32[]{:S(2)}, u32[]{:S(2)}) %collective-permute-start.7) | collective-permute-done | bytes 147488 | tf_op jit(solution)/shard_map/ppermute | solution.py:23
  45.3 2.9 %collective-permute-start.9 = (bf16[1,288,128]{2,1,0:T(8,128)(2,1)S(1)}, bf16[1,288,128]{2,1,0:T(8,128)(2,1)S(1)}, u32[]{:S(2)}, u32[]{:S(2)}) collective-permute-start(bf16[1,288,128]{2,1,0:T(8,128)(2,1)S(1)} %get-tuple-element.57), channel_id=1, source_target_pairs={{0,28},{4,0},{8,4},{12,8},{16,12},{20,16},{24,20},{28,24},{1,29},{... | collective-permute-start | bytes 221192 | tf_op jit(solution)/shard_map/ppermute | solution.py:23
  48.8 1.8 %collective-permute-start.17 = (bf16[1,224,128]{2,1,0:T(8,128)(2,1)S(1)}, bf16[1,224,128]{2,1,0:T(8,128)(2,1)S(1)}, u32[]{:S(2)}, u32[]{:S(2)}) collective-permute-start(bf16[1,224,128]{2,1,0:T(8,128)(2,1)S(1)} %add_convert_fusion.3), channel_id=1, source_target_pairs={{0,3},{1,2},{2,1},{3,0},{4,7},{5,6},{6,5},{7,4},{8,11},{9,10},{10,... | collective-permute-start | bytes 172040 | tf_op jit(solution)/shard_map/ppermute | solution.py:46
  50.6 2.5 %collective-permute-done.17.last_ref = bf16[1,224,128]{2,1,0:T(8,128)(2,1)S(1)} collective-permute-done((bf16[1,224,128]{2,1,0:T(8,128)(2,1)S(1)}, bf16[1,224,128]{2,1,0:T(8,128)(2,1)S(1)}, u32[]{:S(2)}, u32[]{:S(2)}) %collective-permute-start.17) | collective-permute-done | bytes 57376 | tf_op jit(solution)/shard_map/ppermute | solution.py:46
  53.5 1.5 %shard_map.58 = (bf16[512,128]{1,0:T(8,128)(2,1)S(1)}, bf16[128,2,128]{2,1,0:T(2,128)(2,1)}) custom-call(s32[2]{0:T(128)S(1)} %pad_add_fusion.at_ref, s32[16]{0:T(128)S(1)} %copy-done, s32[512,128]{1,0:T(8,128)S(1)} %get-tuple-element.34.block_ref, f32[512,128]{1,0:T(8,128)S(1)} %get-tuple-element.35.scale_ref, ...), custom_call_target="tpu_custom_call" | custom-call | tf_op jit(solution)/shard_map/pallas_call | solution.py:93
  55.0 2.5 %collective-permute-start.20 = (bf16[512,128]{1,0:T(8,128)(2,1)S(1)}, bf16[512,128]{1,0:T(8,128)(2,1)S(1)}, u32[]{:S(2)}, u32[]{:S(2)}) collective-permute-start(bf16[512,128]{1,0:T(8,128)(2,1)S(1)} %get-tuple-element.53), channel_id=1, source_target_pairs={{0,192},{64,128},{128,64},{192,0},{1,193},{65,129},{129,65},{193,1... | collective-permute-start | bytes 393224 | tf_op jit(solution)/shard_map/ppermute | solution.py:46
  61.4 1.4 %collective-permute-done.18 = bf16[512,128]{1,0:T(8,128)(2,1)S(1)} collective-permute-done((bf16[512,128]{1,0:T(8,128)(2,1)S(1)}, bf16[512,128]{1,0:T(8,128)(2,1)S(1)}, u32[]{:S(2)}, u32[]{:S(2)}) %collective-permute-start.18) | collective-permute-done | bytes 131104 | tf_op jit(solution)/shard_map/ppermute | solution.py:46
  62.9 10.0 %collective-permute-start.21 = (f32[512,128]{1,0:T(8,128)S(1)}, f32[512,128]{1,0:T(8,128)S(1)}, u32[]{:S(2)}, u32[]{:S(2)}) collective-permute-start(f32[512,128]{1,0:T(8,128)S(1)} %add_add_fusion), channel_id=1, source_target_pairs={{0,32},{32,0},{1,33},{33,1},{2,34},{34,2},{3,35},{35,3},{4,36},{36... | collective-permute-start | bytes 786440 | tf_op jit(solution)/shard_map/ppermute | solution.py:23
  72.9 11.6 %all-to-all-start = ((bf16[128,2,128]{2,1,0:T(2,128)(2,1)}), bf16[128,2,128]{2,1,0:T(2,128)(2,1)S(1)}, u32[]{:S(2)}, u32[]{:S(2)}) async-start(bf16[128,2,128]{2,1,0:T(2,128)(2,1)} %get-tuple-element.52), calls=%async_computation | async-start | bytes 131072 | tf_op jit(solution)/shard_map/all_to_all | solution.py:199
  85.2 9.9 %all-to-all-done = bf16[128,2,128]{2,1,0:T(2,128)(2,1)S(1)} async-done(((bf16[128,2,128]{2,1,0:T(2,128)(2,1)}), bf16[128,2,128]{2,1,0:T(2,128)(2,1)S(1)}, u32[]{:S(2)}, u32[]{:S(2)}) %all-to-all-start) | async-done | bytes 65568 | tf_op jit(solution)/shard_map/all_to_all | solution.py:199
  95.2 1.5 %collective-permute-start.22 = (bf16[2,128]{1,0:T(2,128)(2,1)S(1)}, bf16[2,128]{1,0:T(2,128)(2,1)S(1)}, u32[]{:S(2)}, u32[]{:S(2)}) collective-permute-start(bf16[2,128]{1,0:T(2,128)(2,1)S(1)} %reduce_max.18), channel_id=1, source_target_pairs={{0,32},{32,0},{1,33},{33,1},{2,34},{34,2},{3,35},{35,3},{4,36},{36... | collective-permute-start | bytes 1544 | tf_op jit(solution)/shard_map/ppermute | solution.py:23
  (45 shorter events, 19.2 us)
Async XLA Ops:
  2.5 8.4 %collective-permute-start.3 = (bf16[4,288,128]{2,1,0:T(8,128)(2,1)S(1)}, bf16[4,288,128]{2,1,0:T(8,128)(2,1)S(1)}, u32[]{:S(2)}, u32[]{:S(2)}) collective-permute-start(bf16[4,288,128]{2,1,0:T(8,128)(2,1)S(1)} %get-tuple-element.36), channel_id=1, source_target_pairs={{0,1},{1,2},{2,3},{3,0},{4,5},{5,6},{6,7},{7,4},{8,9},{9,10},{10,1... | collective-permute-start | bytes 884744 | tf_op jit(solution)/shard_map/ppermute | solution.py:23
  4.7 7.4 %collective-permute-start.4 = (bf16[4,288,128]{2,1,0:T(8,128)(2,1)S(1)}, bf16[4,288,128]{2,1,0:T(8,128)(2,1)S(1)}, u32[]{:S(2)}, u32[]{:S(2)}) collective-permute-start(bf16[4,288,128]{2,1,0:T(8,128)(2,1)S(1)} %get-tuple-element.37), channel_id=1, source_target_pairs={{0,3},{1,0},{2,1},{3,2},{4,7},{5,4},{6,5},{7,6},{8,11},{9,8},{10,9... | collective-permute-start | bytes 884744 | tf_op jit(solution)/shard_map/ppermute | solution.py:23
  6.2 9.3 %collective-permute-start = (bf16[4,224,128]{2,1,0:T(8,128)(2,1)S(1)}, bf16[4,224,128]{2,1,0:T(8,128)(2,1)S(1)}, u32[]{:S(2)}, u32[]{:S(2)}) collective-permute-start(bf16[4,224,128]{2,1,0:T(8,128)(2,1)S(1)} %get-tuple-element.29), channel_id=1, source_target_pairs={{0,4},{4,0},{8,12},{12,8},{16,20},{20,16},{24,28},{28,24},{1,5},{5... | collective-permute-start | bytes 688136 | tf_op jit(solution)/shard_map/ppermute | solution.py:46
  12.8 23.9 %collective-permute-start.5 = (bf16[8,288,128]{2,1,0:T(8,128)(2,1)S(1)}, bf16[8,288,128]{2,1,0:T(8,128)(2,1)S(1)}, u32[]{:S(2)}, u32[]{:S(2)}) collective-permute-start(bf16[8,288,128]{2,1,0:T(8,128)(2,1)S(1)} %get-tuple-element.38), channel_id=1, source_target_pairs={{0,1},{1,2},{2,3},{3,0},{4,5},{5,6},{6,7},{7,4},{8,9},{9,10},{10,1... | collective-permute-start | bytes 1769480 | tf_op jit(solution)/shard_map/ppermute | solution.py:23
  14.4 22.3 %collective-permute-start.6 = (bf16[8,288,128]{2,1,0:T(8,128)(2,1)S(1)}, bf16[8,288,128]{2,1,0:T(8,128)(2,1)S(1)}, u32[]{:S(2)}, u32[]{:S(2)}) collective-permute-start(bf16[8,288,128]{2,1,0:T(8,128)(2,1)S(1)} %get-tuple-element.39), channel_id=1, source_target_pairs={{0,3},{1,0},{2,1},{3,2},{4,7},{5,4},{6,5},{7,6},{8,11},{9,8},{10,9... | collective-permute-start | bytes 1769480 | tf_op jit(solution)/shard_map/ppermute | solution.py:23
  16.2 10.1 %collective-permute-start.1 = (bf16[4,224,128]{2,1,0:T(8,128)(2,1)S(1)}, bf16[4,224,128]{2,1,0:T(8,128)(2,1)S(1)}, u32[]{:S(2)}, u32[]{:S(2)}) collective-permute-start(bf16[4,224,128]{2,1,0:T(8,128)(2,1)S(1)} %get-tuple-element.30), channel_id=1, source_target_pairs={{0,4},{4,8},{8,12},{12,16},{16,20},{20,24},{24,28},{28,0},{1,5},{5... | collective-permute-start | bytes 688136 | tf_op jit(solution)/shard_map/ppermute | solution.py:23
  18.5 7.9 %collective-permute-start.2 = (bf16[4,224,128]{2,1,0:T(8,128)(2,1)S(1)}, bf16[4,224,128]{2,1,0:T(8,128)(2,1)S(1)}, u32[]{:S(2)}, u32[]{:S(2)}) collective-permute-start(bf16[4,224,128]{2,1,0:T(8,128)(2,1)S(1)} %get-tuple-element.31), channel_id=1, source_target_pairs={{0,28},{4,0},{8,4},{12,8},{16,12},{20,16},{24,20},{28,24},{1,29},{... | collective-permute-start | bytes 688136 | tf_op jit(solution)/shard_map/ppermute | solution.py:23
  27.0 6.2 %collective-permute-start.12 = (bf16[4,224,128]{2,1,0:T(8,128)(2,1)S(1)}, bf16[4,224,128]{2,1,0:T(8,128)(2,1)S(1)}, u32[]{:S(2)}, u32[]{:S(2)}) collective-permute-start(bf16[4,224,128]{2,1,0:T(8,128)(2,1)S(1)} %get-tuple-element.46), channel_id=1, source_target_pairs={{0,4},{4,8},{8,12},{12,16},{16,20},{20,24},{24,28},{28,0},{1,5},{5... | collective-permute-start | bytes 688136 | tf_op jit(solution)/shard_map/ppermute | solution.py:23
  27.1 6.1 %collective-permute-start.13 = (bf16[4,224,128]{2,1,0:T(8,128)(2,1)S(1)}, bf16[4,224,128]{2,1,0:T(8,128)(2,1)S(1)}, u32[]{:S(2)}, u32[]{:S(2)}) collective-permute-start(bf16[4,224,128]{2,1,0:T(8,128)(2,1)S(1)} %get-tuple-element.47), channel_id=1, source_target_pairs={{0,28},{4,0},{8,4},{12,8},{16,12},{20,16},{24,20},{28,24},{1,29},{... | collective-permute-start | bytes 688136 | tf_op jit(solution)/shard_map/ppermute | solution.py:23
  33.9 6.4 %collective-permute-start.14 = (bf16[4,224,128]{2,1,0:T(8,128)(2,1)S(1)}, bf16[4,224,128]{2,1,0:T(8,128)(2,1)S(1)}, u32[]{:S(2)}, u32[]{:S(2)}) collective-permute-start(bf16[4,224,128]{2,1,0:T(8,128)(2,1)S(1)} %get-tuple-element.48), channel_id=1, source_target_pairs={{0,4},{4,8},{8,12},{12,16},{16,20},{20,24},{24,28},{28,0},{1,5},{5... | collective-permute-start | bytes 688136 | tf_op jit(solution)/shard_map/ppermute | solution.py:23
  35.9 5.2 %collective-permute-start.15 = (bf16[4,224,128]{2,1,0:T(8,128)(2,1)S(1)}, bf16[4,224,128]{2,1,0:T(8,128)(2,1)S(1)}, u32[]{:S(2)}, u32[]{:S(2)}) collective-permute-start(bf16[4,224,128]{2,1,0:T(8,128)(2,1)S(1)} %get-tuple-element.49), channel_id=1, source_target_pairs={{0,28},{4,0},{8,4},{12,8},{16,12},{20,16},{24,20},{28,24},{1,29},{... | collective-permute-start | bytes 688136 | tf_op jit(solution)/shard_map/ppermute | solution.py:23
  37.5 6.5 %collective-permute-start.7 = (bf16[2,288,128]{2,1,0:T(8,128)(2,1)S(1)}, bf16[2,288,128]{2,1,0:T(8,128)(2,1)S(1)}, u32[]{:S(2)}, u32[]{:S(2)}) collective-permute-start(bf16[2,288,128]{2,1,0:T(8,128)(2,1)S(1)} %get-tuple-element.41), channel_id=1, source_target_pairs={{0,4},{4,8},{8,12},{12,16},{16,20},{20,24},{24,28},{28,0},{1,5},{5... | collective-permute-start | bytes 442376 | tf_op jit(solution)/shard_map/ppermute | solution.py:23
  38.5 5.5 %collective-permute-start.8 = (bf16[2,288,128]{2,1,0:T(8,128)(2,1)S(1)}, bf16[2,288,128]{2,1,0:T(8,128)(2,1)S(1)}, u32[]{:S(2)}, u32[]{:S(2)}) collective-permute-start(bf16[2,288,128]{2,1,0:T(8,128)(2,1)S(1)} %get-tuple-element.43), channel_id=1, source_target_pairs={{0,28},{4,0},{8,4},{12,8},{16,12},{20,16},{24,20},{28,24},{1,29},{... | collective-permute-start | bytes 442376 | tf_op jit(solution)/shard_map/ppermute | solution.py:23
  41.7 7.1 %collective-permute-start.16 = (bf16[2,224,128]{2,1,0:T(8,128)(2,1)S(1)}, bf16[2,224,128]{2,1,0:T(8,128)(2,1)S(1)}, u32[]{:S(2)}, u32[]{:S(2)}) collective-permute-start(bf16[2,224,128]{2,1,0:T(8,128)(2,1)S(1)} %get-tuple-element.51), channel_id=1, source_target_pairs={{0,1},{1,0},{2,3},{3,2},{4,5},{5,4},{6,7},{7,6},{8,9},{9,8},{10,11... | collective-permute-start | bytes 344072 | tf_op jit(solution)/shard_map/ppermute | solution.py:46
  44.1 9.0 %collective-permute-start.11 = (bf16[1,288,128]{2,1,0:T(8,128)(2,1)S(1)}, bf16[1,288,128]{2,1,0:T(8,128)(2,1)S(1)}, u32[]{:S(2)}, u32[]{:S(2)}) collective-permute-start(bf16[1,288,128]{2,1,0:T(8,128)(2,1)S(1)} %get-tuple-element.56), channel_id=1, source_target_pairs={{0,20},{4,24},{8,28},{12,0},{16,4},{20,8},{24,12},{28,16},{1,21},{... | collective-permute-start | bytes 221192 | tf_op jit(solution)/shard_map/ppermute | solution.py:23
  45.3 7.8 %collective-permute-start.9 = (bf16[1,288,128]{2,1,0:T(8,128)(2,1)S(1)}, bf16[1,288,128]{2,1,0:T(8,128)(2,1)S(1)}, u32[]{:S(2)}, u32[]{:S(2)}) collective-permute-start(bf16[1,288,128]{2,1,0:T(8,128)(2,1)S(1)} %get-tuple-element.57), channel_id=1, source_target_pairs={{0,28},{4,0},{8,4},{12,8},{16,12},{20,16},{24,20},{28,24},{1,29},{... | collective-permute-start | bytes 221192 | tf_op jit(solution)/shard_map/ppermute | solution.py:23
  48.2 5.3 %collective-permute-start.10 = (bf16[1,288,128]{2,1,0:T(8,128)(2,1)S(1)}, bf16[1,288,128]{2,1,0:T(8,128)(2,1)S(1)}, u32[]{:S(2)}, u32[]{:S(2)}) collective-permute-start(bf16[1,288,128]{2,1,0:T(8,128)(2,1)S(1)} %get-tuple-element.58), channel_id=1, source_target_pairs={{0,8},{4,12},{8,16},{12,20},{16,24},{20,28},{24,0},{28,4},{1,9},{5... | collective-permute-start | bytes 221192 | tf_op jit(solution)/shard_map/ppermute | solution.py:23
  48.8 4.3 %collective-permute-start.17 = (bf16[1,224,128]{2,1,0:T(8,128)(2,1)S(1)}, bf16[1,224,128]{2,1,0:T(8,128)(2,1)S(1)}, u32[]{:S(2)}, u32[]{:S(2)}) collective-permute-start(bf16[1,224,128]{2,1,0:T(8,128)(2,1)S(1)} %add_convert_fusion.3), channel_id=1, source_target_pairs={{0,3},{1,2},{2,1},{3,0},{4,7},{5,6},{6,5},{7,4},{8,11},{9,10},{10,... | collective-permute-start | bytes 172040 | tf_op jit(solution)/shard_map/ppermute | solution.py:46
  55.0 5.0 %collective-permute-start.20 = (bf16[512,128]{1,0:T(8,128)(2,1)S(1)}, bf16[512,128]{1,0:T(8,128)(2,1)S(1)}, u32[]{:S(2)}, u32[]{:S(2)}) collective-permute-start(bf16[512,128]{1,0:T(8,128)(2,1)S(1)} %get-tuple-element.53), channel_id=1, source_target_pairs={{0,192},{64,128},{128,64},{192,0},{1,193},{65,129},{129,65},{193,1... | collective-permute-start | bytes 393224 | tf_op jit(solution)/shard_map/ppermute | solution.py:46
  57.5 3.9 %collective-permute-start.19 = (bf16[512,128]{1,0:T(8,128)(2,1)S(1)}, bf16[512,128]{1,0:T(8,128)(2,1)S(1)}, u32[]{:S(2)}, u32[]{:S(2)}) collective-permute-start(bf16[512,128]{1,0:T(8,128)(2,1)S(1)} %get-tuple-element.53), channel_id=1, source_target_pairs={{0,64},{64,0},{128,192},{192,128},{1,65},{65,1},{129,193},{193,129... | collective-permute-start | bytes 393224 | tf_op jit(solution)/shard_map/ppermute | solution.py:46
  57.5 5.3 %collective-permute-start.18 = (bf16[512,128]{1,0:T(8,128)(2,1)S(1)}, bf16[512,128]{1,0:T(8,128)(2,1)S(1)}, u32[]{:S(2)}, u32[]{:S(2)}) collective-permute-start(bf16[512,128]{1,0:T(8,128)(2,1)S(1)} %get-tuple-element.53), channel_id=1, source_target_pairs={{0,128},{64,192},{128,0},{192,64},{1,129},{65,193},{129,1},{193,65... | collective-permute-start | bytes 393224 | tf_op jit(solution)/shard_map/ppermute | solution.py:46
  62.9 21.6 %collective-permute-start.21 = (f32[512,128]{1,0:T(8,128)S(1)}, f32[512,128]{1,0:T(8,128)S(1)}, u32[]{:S(2)}, u32[]{:S(2)}) collective-permute-start(f32[512,128]{1,0:T(8,128)S(1)} %add_add_fusion), channel_id=1, source_target_pairs={{0,32},{32,0},{1,33},{33,1},{2,34},{34,2},{3,35},{35,3},{4,36},{36... | collective-permute-start | bytes 786440 | tf_op jit(solution)/shard_map/ppermute | solution.py:23
  72.9 22.2 %all-to-all-start = ((bf16[128,2,128]{2,1,0:T(2,128)(2,1)}), bf16[128,2,128]{2,1,0:T(2,128)(2,1)S(1)}, u32[]{:S(2)}, u32[]{:S(2)}) async-start(bf16[128,2,128]{2,1,0:T(2,128)(2,1)} %get-tuple-element.52), calls=%async_computation | async-start | bytes 131072 | tf_op jit(solution)/shard_map/all_to_all | solution.py:199
  95.2 2.3 %collective-permute-start.22 = (bf16[2,128]{1,0:T(2,128)(2,1)S(1)}, bf16[2,128]{1,0:T(2,128)(2,1)S(1)}, u32[]{:S(2)}, u32[]{:S(2)}) collective-permute-start(bf16[2,128]{1,0:T(2,128)(2,1)S(1)} %reduce_max.18), channel_id=1, source_target_pairs={{0,32},{32,0},{1,33},{33,1},{2,34},{34,2},{3,35},{35,3},{4,36},{36... | collective-permute-start | bytes 1544 | tf_op jit(solution)/shard_map/ppermute | solution.py:23
  (2 other events, 23.8 us)

commit v2 on v1

--- a/solution.py
+++ b/solution.py
@@ -55,9 +55,9 @@
 SMALL = pltpu.CompilerParams(vmem_limit_bytes=8 << 20)
 
 
-def prepare_kernel(at_ref, len_ref, hist_ref, block_ref, scale_ref):
+def prepare_kernel(len_ref, hist_ref, block_ref, scale_ref):
     position = (
-        (at_ref[0] * 4 + at_ref[1]) * (ROWS * 128)
+        (lax.axis_index("z") * 4 + lax.axis_index("y")) * (ROWS * 128)
         + lax.broadcasted_iota(jnp.int32, (ROWS, 128), 0) * 128
         + lax.broadcasted_iota(jnp.int32, (ROWS, 128), 1)
     )
@@ -75,41 +75,41 @@
     scale_ref[...] = scale
 
 
-def prepare(at, block_len, amax_history):
+def prepare(block_len, amax_history):
     return pl.pallas_call(
         prepare_kernel,
         out_shape=(
             jax.ShapeDtypeStruct((ROWS, 128), jnp.int32),
             jax.ShapeDtypeStruct((ROWS, 128), jnp.float32),
         ),
-        in_specs=[SMEM, SMEM, VMEM],
+        in_specs=[SMEM, VMEM],
         out_specs=[VMEM] * 2,
         name="prepare",
         compiler_params=SMALL,
-    )(at, block_len, amax_history)
-
-
-def call(kernel, out, at, *arrays, scratch=()):
+    )(block_len, amax_history)
+
+
+def call(kernel, out, *arrays, scratch=()):
     made = pl.pallas_call(
         kernel,
         out_shape=[pltpu.VMEM(shape, jnp.bfloat16) for shape in out],
-        in_specs=[SMEM] + [SMEM if a.ndim == 1 else VMEM for a in arrays],
+        in_specs=[VMEM] * len(arrays),
         out_specs=[VMEM] * len(out),
         scratch_shapes=scratch,
         compiler_params=SMALL,
-    )(at, *[a if a.ndim == 1 else in_vmem(a) for a in arrays])
+    )(*[in_vmem(a) for a in arrays])
     return made
 
 
-def copied(body, out, at, g):
+def copied(body, name, out, g):
     return pl.pallas_call(
         body,
         out_shape=[pltpu.VMEM(shape, jnp.bfloat16) for shape in out],
-        in_specs=[SMEM, pl.BlockSpec(memory_space=pltpu.HBM)],
+        in_specs=[pl.BlockSpec(memory_space=pl.ANY if name == "stage" else pltpu.HBM)],
         out_specs=[VMEM] * len(out),
         scratch_shapes=[pltpu.SemaphoreType.DMA((8,))],
         compiler_params=SMALL,
-    )(at, pltpu.with_memory_space_constraint(g, pltpu.HBM))
+    )(g if name == "stage" else pltpu.with_memory_space_constraint(g, pltpu.HBM))
 
 
 def run_copies(sems, pairs):
@@ -120,8 +120,8 @@
         copy.wait()
 
 
-def open_kernel(at_ref, g_ref, far_z_ref, up_ref, down_ref, sems):
-    z, y = at_ref[0], at_ref[1]
+def open_kernel(g_ref, far_z_ref, up_ref, down_ref, sems):
+    z, y = lax.axis_index("z"), lax.axis_index("y")
     row = (y + 2) % 4
     run_copies(sems, [
         (g_ref.at[(z + 4) % 8, :, A:], far_z_ref),
@@ -130,33 +130,33 @@
     ])
 
 
-def stage_kernel(at_ref, g_ref, out_ref, sems):
+def stage_kernel(g_ref, out_ref, sems):
     run_copies(sems, [(g_ref.at[i], out_ref.at[i]) for i in range(8)])
 
 
-def b_first_kernel(at_ref, g_ref, got_ref, up_ref, down_ref):
-    z = at_ref[0]
+def b_first_kernel(g_ref, got_ref, up_ref, down_ref):
+    z = lax.axis_index("z")
     odd = (z % 2).astype(jnp.float32)
     got = f32(got_ref[...])
     up_ref[...] = bf(f32(g_ref[(z + 3) % 8, :, A:]) + got * odd)
     down_ref[...] = bf(f32(g_ref[(z + 5) % 8, :, A:]) + got * (1.0 - odd))
 
 
-def b_next_kernel(by, at_ref, g_ref, got_up_ref, got_down_ref, up_ref, down_ref):
-    z = at_ref[0]
+def b_next_kernel(by, g_ref, got_up_ref, got_down_ref, up_ref, down_ref):
+    z = lax.axis_index("z")
     up_ref[...] = bf(add(g_ref[(z + by) % 8, :, A:], got_up_ref[...]))
     down_ref[...] = bf(add(g_ref[(z + 8 - by) % 8, :, A:], got_down_ref[...]))
 
 
-def b_last_kernel(at_ref, g_ref, got_up_ref, got_down_ref, keep_ref, give_ref):
-    z, y = at_ref[0], at_ref[1]
+def b_last_kernel(g_ref, got_up_ref, got_down_ref, keep_ref, give_ref):
+    z, y = lax.axis_index("z"), lax.axis_index("y")
     other = y + 1 - 2 * (y % 2)
     for ref, slot, row in ((keep_ref, 0, y), (keep_ref, 1, 3 - y), (give_ref, 0, other), (give_ref, 1, 3 - other)):
         ref[slot] = bf(add(g_ref[z, row, A:], got_up_ref[row], got_down_ref[row]))
 
 
-def a_first_kernel(at_ref, g_ref, got_up_ref, got_down_ref, up_ref, down_ref):
-    y = at_ref[1]
+def a_first_kernel(g_ref, got_up_ref, got_down_ref, up_ref, down_ref):
+    y = lax.axis_index("y")
     up, down = (y + 1) % 4, (y + 3) % 4
     up_ref[0:4] = bf(add(g_ref[0:4, up, :A], got_up_ref[...]))
     up_ref[4:8] = g_ref[4:8, up, :A]
@@ -164,8 +164,8 @@
     down_ref[4:8] = bf(add(g_ref[4:8, down, :A], got_down_ref[...]))
 
 
-def a_last_kernel(at_ref, g_ref, got_up_ref, got_down_ref, own_ref, up_ref, down_ref, near_ref):
-    z, y = at_ref[0], at_ref[1]
+def a_last_kernel(g_ref, got_up_ref, got_down_ref, own_ref, up_ref, down_ref, near_ref):
+    z, y = lax.axis_index("z"), lax.axis_index("y")
     wanted = ((up_ref, 0, 1), (up_ref, 1, 3), (down_ref, 0, 6), (down_ref, 1, 4))
     wanted += ((near_ref, 0, 7), (near_ref, 1, 5), (near_ref, 2, 2), (own_ref, 0, 0))
     for ref, slot, by in wanted:
@@ -173,16 +173,11 @@
         ref[slot] = bf(add(g_ref[row, y, :A], got_up_ref[row], got_down_ref[row]))
 
 
-def quantize_kernel(at_ref, len_ref, block_ref, scale_ref, pa_ref, rows_ref, one_ref, two_ref, three_ref, pb_ref, half_ref, last_ref, q_ref, m_ref, s_ref):
+def quantize_kernel(block_ref, scale_ref, pa_ref, rows_ref, one_ref, two_ref, three_ref, pb_ref, half_ref, last_ref, q_ref, m_ref, s_ref):
     s_ref[0:A] = add(pa_ref[0], rows_ref[0], one_ref[0], three_ref[0], two_ref[0])
     s_ref[A:ROWS] = add(pb_ref[0], half_ref[0], last_ref[0])
     q_ref[...] = bf(jnp.clip(s_ref[...] * scale_ref[...], -SATURATE, SATURATE))
-    start = (at_ref[0] * 4 + at_ref[1]) * (ROWS * 128)
-    low, high, end = jnp.int32(0), jnp.int32(0), jnp.int32(0)
-    for c in range(BLOCKS - 1):
-        end = end + len_ref[c]
-        low = low + (start >= end).astype(jnp.int32)
-        high = high + (start + (ROWS * 128 - 1) >= end).astype(jnp.int32)
+    low, high = block_ref[0, 0], block_ref[ROWS - 1, 127]
     lane = lax.broadcasted_iota(jnp.int32, (8, 128), 1)
 
     def one_tensor(c, tops):
@@ -209,31 +204,28 @@
 
 def body(gradients, block_len, amax_history):
     g = gradients.reshape(8, 4, ROWS, 128)
-    z, y = lax.axis_index("z"), lax.axis_index("y")
-    at = jnp.stack([z, y]).astype(jnp.int32)
-
     four_z, eight_z, four_y = (4, B, 128), (8, A, 128), (2, A, 128)
-    got, a_up, a_dn = copied(open_kernel, (four_z, (4, A, 128), (4, A, 128)), at, g)
+    got, a_up, a_dn = copied(open_kernel, "open", (four_z, (4, A, 128), (4, A, 128)), g)
     got = send(got, "z", 1, swap)
     a_up, a_dn = both_ways(a_up, a_dn, "y")
-    (g,) = copied(stage_kernel, ((8, 4, ROWS, 128),), at, g)
-    b_up, b_dn = call(b_first_kernel, (four_z, four_z), at, g, got)
+    (g,) = copied(stage_kernel, "stage", ((8, 4, ROWS, 128),), g)
+    b_up, b_dn = call(b_first_kernel, (four_z, four_z), g, got)
     b_up, b_dn = both_ways(b_up, b_dn, "z")
-    a_up, a_dn = call(a_first_kernel, (eight_z, eight_z), at, g, a_up, a_dn)
+    a_up, a_dn = call(a_first_kernel, (eight_z, eight_z), g, a_up, a_dn)
     a_up, a_dn = both_ways(a_up, a_dn, "y")
 
-    block, scale = prepare(at, block_len, amax_history)
+    b_up, b_dn = call(functools.partial(b_next_kernel, 2), (four_z, four_z), g, b_up, b_dn)
+    b_up, b_dn, block_len = together(b_up, b_dn, block_len)
+    b_up, b_dn = both_ways(b_up, b_dn, "z")
+    block, scale = prepare(block_len, amax_history)
     b_up, b_dn, block, scale = together(b_up, b_dn, block, scale)
-
-    b_up, b_dn = call(functools.partial(b_next_kernel, 2), (four_z, four_z), at, g, b_up, b_dn)
+    b_up, b_dn = call(functools.partial(b_next_kernel, 1), (four_z, four_z), g, b_up, b_dn)
     b_up, b_dn = both_ways(b_up, b_dn, "z")
-    b_up, b_dn = call(functools.partial(b_next_kernel, 1), (four_z, four_z), at, g, b_up, b_dn)
-    b_up, b_dn = both_ways(b_up, b_dn, "z")
-
-    pa, a_up, a_dn, near = call(a_last_kernel, ((1, A, 128), four_y, four_y, (3, A, 128)), at, g, a_up, a_dn)
+
+    pa, a_up, a_dn, near = call(a_last_kernel, ((1, A, 128), four_y, four_y, (3, A, 128)), g, a_up, a_dn)
     a_up, a_dn = both_ways(a_up, a_dn, "z")
     half = (2, B, 128)
-    pb, half = call(b_last_kernel, (half, half), at, g, b_up, b_dn)
+    pb, half = call(b_last_kernel, (half, half), g, b_up, b_dn)
     half = send(half, "y", 1, swap)
 
     a_three = send(bf(add(near[1:2], a_dn[1:2])), "z", -3)
@@ -244,7 +236,7 @@
 
     q, m = call(
         quantize_kernel, ((ROWS, 128), (DEVICES // 2, 2, 128)),
-        at, block_len, block, scale, pa, a_up, a_one, a_two, a_three, pb, half, last,
+        block, scale, pa, a_up, a_one, a_two, a_three, pb, half, last,
         scratch=[pltpu.VMEM((ROWS, 128), jnp.float32)],
     )
 

time: 98.2 us -> 94.7 us (0.964)
  Pallas kernels: 11.3 us -> 4.75 us
  waiting for transfers between devices: 28.1 us -> 31.1 us
    pallas_call x7, Pallas kernels: 5.55 us -> 1.78 us  [call(): pl.pallas_call(kernel, out_shape=[pltpu.VMEM(shape, jnp.bfloat16) for sha...]
    pallas_call x2, Pallas kernels: 4.55 us -> 1.76 us  [copied(): pl.pallas_call(body, out_shape=[pltpu.VMEM(shape, jnp.bfloat16) for shape...]
    ppermute x17, waiting for transfers between devices: 11.8 us -> 14 us  [shift(): return lax.ppermute(x, axis, [(i, (i + by) % n) for i in range(n)])]
    ppermute x17, starting transfers between devices: 37.3 us -> 38.4 us  [shift(): return lax.ppermute(x, axis, [(i, (i + by) % n) for i in range(n)])]
  transfers between devices with their start and end apart: 24 -> 24, of which waited for: 13 -> 14; matrix products, arithmetic and copies ran while one was open for 1% -> 1% of each run, Pallas kernels for 8% -> 3%
where the time goes in v2:
time: 94.7 us; the launch traced here: 94.6 us
  starting transfers between devices  56.4 us (60%)
  waiting for transfers between devices  31.1 us (33%)
  Pallas kernels  4.75 us (5%)
  other arithmetic  1.53 us (2%)
    ppermute x17, starting transfers between devices, shift(): return lax.ppermute(x, axis, [(i, (i + by) % n) for i in range(n)])  38.4 us
    ppermute x17, waiting for transfers between devices, shift(): return lax.ppermute(x, axis, [(i, (i + by) % n) for i in range(n)])  14 us
    all_to_all x1, starting transfers between devices, exchange(): return lax.all_to_all(x, axes, split_axis=0, concat_axis=0, tiled=True)  11.1 us
    all_to_all x1, waiting for transfers between devices, exchange(): return lax.all_to_all(x, axes, split_axis=0, concat_axis=0, tiled=True)  9.86 us
    ppermute x6, waiting for transfers between devices, swap(): return lax.ppermute(x, axis, [(i, i ^ by) for i in range(SIZE[axis])])  7.28 us
    ppermute x6, starting transfers between devices, swap(): return lax.ppermute(x, axis, [(i, i ^ by) for i in range(SIZE[axis])])  6.97 us
  transfers between devices with their start and end apart: 24, of which 14 were waited for; matrix products, arithmetic and copies ran while one was open for 1% of the time, Pallas kernels for 3%

profile of v2, /device:TPU:1, one launch (start us, length us, event | category | flops | bytes accessed | tf_op | source)
XLA Modules:
  0.0 94.6 jit_solution(13668482854456999920)
XLA Ops:
  0.6 1.4 %shard_map.51 = (bf16[4,224,128]{2,1,0:T(8,128)(2,1)S(1)}, bf16[4,288,128]{2,1,0:T(8,128)(2,1)S(1)}, bf16[4,288,128]{2,1,0:T(8,128)(2,1)S(1)}) custom-call(bf16[8,4,512,128]{3,2,1,0:T(8,128)(2,1)} %bitcast.2), custom_call_target="tpu_custom_call" | custom-call | tf_op jit(solution)/shard_map/pallas_call | solution.py:105
  2.0 2.2 %collective-permute-start.5 = (bf16[4,288,128]{2,1,0:T(8,128)(2,1)S(1)}, bf16[4,288,128]{2,1,0:T(8,128)(2,1)S(1)}, u32[]{:S(2)}, u32[]{:S(2)}) collective-permute-start(bf16[4,288,128]{2,1,0:T(8,128)(2,1)S(1)} %get-tuple-element.44), channel_id=1, source_target_pairs={{0,1},{1,2},{2,3},{3,0},{4,5},{5,6},{6,7},{7,4},{8,9},{9,10},{10,1... | collective-permute-start | bytes 884744 | tf_op jit(solution)/shard_map/ppermute | solution.py:23
  4.2 1.5 %collective-permute-start.6 = (bf16[4,288,128]{2,1,0:T(8,128)(2,1)S(1)}, bf16[4,288,128]{2,1,0:T(8,128)(2,1)S(1)}, u32[]{:S(2)}, u32[]{:S(2)}) collective-permute-start(bf16[4,288,128]{2,1,0:T(8,128)(2,1)S(1)} %get-tuple-element.45), channel_id=1, source_target_pairs={{0,3},{1,0},{2,1},{3,2},{4,7},{5,4},{6,5},{7,6},{8,11},{9,8},{10,9... | collective-permute-start | bytes 884744 | tf_op jit(solution)/shard_map/ppermute | solution.py:23
  5.8 1.6 %collective-permute-start = (bf16[4,224,128]{2,1,0:T(8,128)(2,1)S(1)}, bf16[4,224,128]{2,1,0:T(8,128)(2,1)S(1)}, u32[]{:S(2)}, u32[]{:S(2)}) collective-permute-start(bf16[4,224,128]{2,1,0:T(8,128)(2,1)S(1)} %get-tuple-element.32), channel_id=1, source_target_pairs={{0,4},{4,0},{8,12},{12,8},{16,20},{20,16},{24,28},{28,24},{1,5},{5... | collective-permute-start | bytes 688136 | tf_op jit(solution)/shard_map/ppermute | solution.py:46
  7.8 2.7 %collective-permute-done.5.got_up_ref = bf16[4,288,128]{2,1,0:T(8,128)(2,1)S(1)} collective-permute-done((bf16[4,288,128]{2,1,0:T(8,128)(2,1)S(1)}, bf16[4,288,128]{2,1,0:T(8,128)(2,1)S(1)}, u32[]{:S(2)}, u32[]{:S(2)}) %collective-permute-start.5) | collective-permute-done | bytes 294944 | tf_op jit(solution)/shard_map/ppermute | solution.py:23
  11.8 1.6 %collective-permute-start.7 = (bf16[8,288,128]{2,1,0:T(8,128)(2,1)S(1)}, bf16[8,288,128]{2,1,0:T(8,128)(2,1)S(1)}, u32[]{:S(2)}, u32[]{:S(2)}) collective-permute-start(bf16[8,288,128]{2,1,0:T(8,128)(2,1)S(1)} %get-tuple-element.46), channel_id=1, source_target_pairs={{0,1},{1,2},{2,3},{3,0},{4,5},{5,6},{6,7},{7,4},{8,9},{9,10},{10,1... | collective-permute-start | bytes 1769480 | tf_op jit(solution)/shard_map/ppermute | solution.py:23
  14.7 2.3 %collective-permute-start.1 = (bf16[4,224,128]{2,1,0:T(8,128)(2,1)S(1)}, bf16[4,224,128]{2,1,0:T(8,128)(2,1)S(1)}, u32[]{:S(2)}, u32[]{:S(2)}) collective-permute-start(bf16[4,224,128]{2,1,0:T(8,128)(2,1)S(1)} %get-tuple-element.33), channel_id=1, source_target_pairs={{0,4},{4,8},{8,12},{12,16},{16,20},{20,24},{24,28},{28,0},{1,5},{5... | collective-permute-start | bytes 688136 | tf_op jit(solution)/shard_map/ppermute | solution.py:23
  17.0 4.0 %collective-permute-start.2 = (bf16[4,224,128]{2,1,0:T(8,128)(2,1)S(1)}, bf16[4,224,128]{2,1,0:T(8,128)(2,1)S(1)}, u32[]{:S(2)}, u32[]{:S(2)}) collective-permute-start(bf16[4,224,128]{2,1,0:T(8,128)(2,1)S(1)} %get-tuple-element.34), channel_id=1, source_target_pairs={{0,28},{4,0},{8,4},{12,8},{16,12},{20,16},{24,20},{28,24},{1,29},{... | collective-permute-start | bytes 688136 | tf_op jit(solution)/shard_map/ppermute | solution.py:23
  21.0 3.8 %collective-permute-done.1.got_up_ref = bf16[4,224,128]{2,1,0:T(8,128)(2,1)S(1)} collective-permute-done((bf16[4,224,128]{2,1,0:T(8,128)(2,1)S(1)}, bf16[4,224,128]{2,1,0:T(8,128)(2,1)S(1)}, u32[]{:S(2)}, u32[]{:S(2)}) %collective-permute-start.1) | collective-permute-done | bytes 229408 | tf_op jit(solution)/shard_map/ppermute | solution.py:23
  25.1 2.7 %collective-permute-start.4 = (bf16[4,224,128]{2,1,0:T(8,128)(2,1)S(1)}, bf16[4,224,128]{2,1,0:T(8,128)(2,1)S(1)}, u32[]{:S(2)}, u32[]{:S(2)}) collective-permute-start(bf16[4,224,128]{2,1,0:T(8,128)(2,1)S(1)} %get-tuple-element.38), channel_id=1, source_target_pairs={{0,28},{4,0},{8,4},{12,8},{16,12},{20,16},{24,20},{28,24},{1,29},{... | collective-permute-start | bytes 688136 | tf_op jit(solution)/shard_map/ppermute | solution.py:23
  28.9 2.2 %collective-permute-done.3.got_up_ref = bf16[4,224,128]{2,1,0:T(8,128)(2,1)S(1)} collective-permute-done((bf16[4,224,128]{2,1,0:T(8,128)(2,1)S(1)}, bf16[4,224,128]{2,1,0:T(8,128)(2,1)S(1)}, u32[]{:S(2)}, u32[]{:S(2)}) %collective-permute-start.3) | collective-permute-done | bytes 229408 | tf_op jit(solution)/shard_map/ppermute | solution.py:23
  31.2 2.0 %collective-permute-start.14 = (bf16[4,224,128]{2,1,0:T(8,128)(2,1)S(1)}, bf16[4,224,128]{2,1,0:T(8,128)(2,1)S(1)}, u32[]{:S(2)}, u32[]{:S(2)}) collective-permute-start(bf16[4,224,128]{2,1,0:T(8,128)(2,1)S(1)} %get-tuple-element.54), channel_id=1, source_target_pairs={{0,4},{4,8},{8,12},{12,16},{16,20},{20,24},{24,28},{28,0},{1,5},{5... | collective-permute-start | bytes 688136 | tf_op jit(solution)/shard_map/ppermute | solution.py:23
  35.4 2.0 %collective-permute-start.10 = (bf16[2,288,128]{2,1,0:T(8,128)(2,1)S(1)}, bf16[2,288,128]{2,1,0:T(8,128)(2,1)S(1)}, u32[]{:S(2)}, u32[]{:S(2)}) collective-permute-start(bf16[2,288,128]{2,1,0:T(8,128)(2,1)S(1)} %get-tuple-element.51), channel_id=1, source_target_pairs={{0,28},{4,0},{8,4},{12,8},{16,12},{20,16},{24,20},{28,24},{1,29},{... | collective-permute-start | bytes 442376 | tf_op jit(solution)/shard_map/ppermute | solution.py:23
  38.8 2.1 %collective-permute-done.9.rows_ref = bf16[2,288,128]{2,1,0:T(8,128)(2,1)S(1)} collective-permute-done((bf16[2,288,128]{2,1,0:T(8,128)(2,1)S(1)}, bf16[2,288,128]{2,1,0:T(8,128)(2,1)S(1)}, u32[]{:S(2)}, u32[]{:S(2)}) %collective-permute-start.9) | collective-permute-done | bytes 147488 | tf_op jit(solution)/shard_map/ppermute | solution.py:23
  42.2 2.4 %collective-permute-start.11 = (bf16[1,288,128]{2,1,0:T(8,128)(2,1)S(1)}, bf16[1,288,128]{2,1,0:T(8,128)(2,1)S(1)}, u32[]{:S(2)}, u32[]{:S(2)}) collective-permute-start(bf16[1,288,128]{2,1,0:T(8,128)(2,1)S(1)} %get-tuple-element.63), channel_id=1, source_target_pairs={{0,28},{4,0},{8,4},{12,8},{16,12},{20,16},{24,20},{28,24},{1,29},{... | collective-permute-start | bytes 221192 | tf_op jit(solution)/shard_map/ppermute | solution.py:23
  46.7 3.1 %collective-permute-done.17.last_ref = bf16[1,224,128]{2,1,0:T(8,128)(2,1)S(1)} collective-permute-done((bf16[1,224,128]{2,1,0:T(8,128)(2,1)S(1)}, bf16[1,224,128]{2,1,0:T(8,128)(2,1)S(1)}, u32[]{:S(2)}, u32[]{:S(2)}) %collective-permute-start.17) | collective-permute-done | bytes 57376 | tf_op jit(solution)/shard_map/ppermute | solution.py:46
  50.8 2.5 %collective-permute-start.20 = (bf16[512,128]{1,0:T(8,128)(2,1)S(1)}, bf16[512,128]{1,0:T(8,128)(2,1)S(1)}, u32[]{:S(2)}, u32[]{:S(2)}) collective-permute-start(bf16[512,128]{1,0:T(8,128)(2,1)S(1)} %get-tuple-element.59), channel_id=1, source_target_pairs={{0,192},{64,128},{128,64},{192,0},{1,193},{65,129},{129,65},{193,1... | collective-permute-start | bytes 393224 | tf_op jit(solution)/shard_map/ppermute | solution.py:46
  53.3 1.4 %collective-permute-start.18 = (bf16[512,128]{1,0:T(8,128)(2,1)S(1)}, bf16[512,128]{1,0:T(8,128)(2,1)S(1)}, u32[]{:S(2)}, u32[]{:S(2)}) collective-permute-start(bf16[512,128]{1,0:T(8,128)(2,1)S(1)} %get-tuple-element.59), channel_id=1, source_target_pairs={{0,128},{64,192},{128,0},{192,64},{1,129},{65,193},{129,1},{193,65... | collective-permute-start | bytes 393224 | tf_op jit(solution)/shard_map/ppermute | solution.py:46
  54.7 1.2 %collective-permute-done.20 = bf16[512,128]{1,0:T(8,128)(2,1)S(1)} collective-permute-done((bf16[512,128]{1,0:T(8,128)(2,1)S(1)}, bf16[512,128]{1,0:T(8,128)(2,1)S(1)}, u32[]{:S(2)}, u32[]{:S(2)}) %collective-permute-start.20) | collective-permute-done | bytes 131104 | tf_op jit(solution)/shard_map/ppermute | solution.py:46
  57.1 1.7 %collective-permute-done.18 = bf16[512,128]{1,0:T(8,128)(2,1)S(1)} collective-permute-done((bf16[512,128]{1,0:T(8,128)(2,1)S(1)}, bf16[512,128]{1,0:T(8,128)(2,1)S(1)}, u32[]{:S(2)}, u32[]{:S(2)}) %collective-permute-start.18) | collective-permute-done | bytes 131104 | tf_op jit(solution)/shard_map/ppermute | solution.py:46
  58.9 11.0 %collective-permute-start.21 = (f32[512,128]{1,0:T(8,128)S(1)}, f32[512,128]{1,0:T(8,128)S(1)}, u32[]{:S(2)}, u32[]{:S(2)}) collective-permute-start(f32[512,128]{1,0:T(8,128)S(1)} %add_add_fusion), channel_id=1, source_target_pairs={{0,32},{32,0},{1,33},{33,1},{2,34},{34,2},{3,35},{35,3},{4,36},{36... | collective-permute-start | bytes 786440 | tf_op jit(solution)/shard_map/ppermute | solution.py:23
  69.9 11.1 %all-to-all-start = ((bf16[128,2,128]{2,1,0:T(2,128)(2,1)}), bf16[128,2,128]{2,1,0:T(2,128)(2,1)S(1)}, u32[]{:S(2)}, u32[]{:S(2)}) async-start(bf16[128,2,128]{2,1,0:T(2,128)(2,1)} %get-tuple-element.58), calls=%async_computation | async-start | bytes 131072 | tf_op jit(solution)/shard_map/all_to_all | solution.py:194
  81.7 9.9 %all-to-all-done = bf16[128,2,128]{2,1,0:T(2,128)(2,1)S(1)} async-done(((bf16[128,2,128]{2,1,0:T(2,128)(2,1)}), bf16[128,2,128]{2,1,0:T(2,128)(2,1)S(1)}, u32[]{:S(2)}, u32[]{:S(2)}) %all-to-all-start) | async-done | bytes 65568 | tf_op jit(solution)/shard_map/all_to_all | solution.py:194
  91.7 1.6 %collective-permute-start.22 = (bf16[2,128]{1,0:T(2,128)(2,1)S(1)}, bf16[2,128]{1,0:T(2,128)(2,1)S(1)}, u32[]{:S(2)}, u32[]{:S(2)}) collective-permute-start(bf16[2,128]{1,0:T(2,128)(2,1)S(1)} %reduce_max.18), channel_id=1, source_target_pairs={{0,32},{32,0},{1,33},{33,1},{2,34},{34,2},{3,35},{35,3},{4,36},{36... | collective-permute-start | bytes 1544 | tf_op jit(solution)/shard_map/ppermute | solution.py:23
  (46 shorter events, 16.0 us)
Async XLA Ops:
  2.0 8.4 %collective-permute-start.5 = (bf16[4,288,128]{2,1,0:T(8,128)(2,1)S(1)}, bf16[4,288,128]{2,1,0:T(8,128)(2,1)S(1)}, u32[]{:S(2)}, u32[]{:S(2)}) collective-permute-start(bf16[4,288,128]{2,1,0:T(8,128)(2,1)S(1)} %get-tuple-element.44), channel_id=1, source_target_pairs={{0,1},{1,2},{2,3},{3,0},{4,5},{5,6},{6,7},{7,4},{8,9},{9,10},{10,1... | collective-permute-start | bytes 884744 | tf_op jit(solution)/shard_map/ppermute | solution.py:23
  4.2 7.4 %collective-permute-start.6 = (bf16[4,288,128]{2,1,0:T(8,128)(2,1)S(1)}, bf16[4,288,128]{2,1,0:T(8,128)(2,1)S(1)}, u32[]{:S(2)}, u32[]{:S(2)}) collective-permute-start(bf16[4,288,128]{2,1,0:T(8,128)(2,1)S(1)} %get-tuple-element.45), channel_id=1, source_target_pairs={{0,3},{1,0},{2,1},{3,2},{4,7},{5,4},{6,5},{7,6},{8,11},{9,8},{10,9... | collective-permute-start | bytes 884744 | tf_op jit(solution)/shard_map/ppermute | solution.py:23
  5.8 8.8 %collective-permute-start = (bf16[4,224,128]{2,1,0:T(8,128)(2,1)S(1)}, bf16[4,224,128]{2,1,0:T(8,128)(2,1)S(1)}, u32[]{:S(2)}, u32[]{:S(2)}) collective-permute-start(bf16[4,224,128]{2,1,0:T(8,128)(2,1)S(1)} %get-tuple-element.32), channel_id=1, source_target_pairs={{0,4},{4,0},{8,12},{12,8},{16,20},{20,16},{24,28},{28,24},{1,5},{5... | collective-permute-start | bytes 688136 | tf_op jit(solution)/shard_map/ppermute | solution.py:46
  11.8 22.6 %collective-permute-start.7 = (bf16[8,288,128]{2,1,0:T(8,128)(2,1)S(1)}, bf16[8,288,128]{2,1,0:T(8,128)(2,1)S(1)}, u32[]{:S(2)}, u32[]{:S(2)}) collective-permute-start(bf16[8,288,128]{2,1,0:T(8,128)(2,1)S(1)} %get-tuple-element.46), channel_id=1, source_target_pairs={{0,1},{1,2},{2,3},{3,0},{4,5},{5,6},{6,7},{7,4},{8,9},{9,10},{10,1... | collective-permute-start | bytes 1769480 | tf_op jit(solution)/shard_map/ppermute | solution.py:23
  13.4 21.0 %collective-permute-start.8 = (bf16[8,288,128]{2,1,0:T(8,128)(2,1)S(1)}, bf16[8,288,128]{2,1,0:T(8,128)(2,1)S(1)}, u32[]{:S(2)}, u32[]{:S(2)}) collective-permute-start(bf16[8,288,128]{2,1,0:T(8,128)(2,1)S(1)} %get-tuple-element.47), channel_id=1, source_target_pairs={{0,3},{1,0},{2,1},{3,2},{4,7},{5,4},{6,5},{7,6},{8,11},{9,8},{10,9... | collective-permute-start | bytes 1769480 | tf_op jit(solution)/shard_map/ppermute | solution.py:23
  14.7 10.1 %collective-permute-start.1 = (bf16[4,224,128]{2,1,0:T(8,128)(2,1)S(1)}, bf16[4,224,128]{2,1,0:T(8,128)(2,1)S(1)}, u32[]{:S(2)}, u32[]{:S(2)}) collective-permute-start(bf16[4,224,128]{2,1,0:T(8,128)(2,1)S(1)} %get-tuple-element.33), channel_id=1, source_target_pairs={{0,4},{4,8},{8,12},{12,16},{16,20},{20,24},{24,28},{28,0},{1,5},{5... | collective-permute-start | bytes 688136 | tf_op jit(solution)/shard_map/ppermute | solution.py:23
  17.0 7.9 %collective-permute-start.2 = (bf16[4,224,128]{2,1,0:T(8,128)(2,1)S(1)}, bf16[4,224,128]{2,1,0:T(8,128)(2,1)S(1)}, u32[]{:S(2)}, u32[]{:S(2)}) collective-permute-start(bf16[4,224,128]{2,1,0:T(8,128)(2,1)S(1)} %get-tuple-element.34), channel_id=1, source_target_pairs={{0,28},{4,0},{8,4},{12,8},{16,12},{20,16},{24,20},{28,24},{1,29},{... | collective-permute-start | bytes 688136 | tf_op jit(solution)/shard_map/ppermute | solution.py:23
  25.0 6.2 %collective-permute-start.3 = (bf16[4,224,128]{2,1,0:T(8,128)(2,1)S(1)}, bf16[4,224,128]{2,1,0:T(8,128)(2,1)S(1)}, u32[]{:S(2)}, u32[]{:S(2)}) collective-permute-start(bf16[4,224,128]{2,1,0:T(8,128)(2,1)S(1)} %get-tuple-element.37), channel_id=1, source_target_pairs={{0,4},{4,8},{8,12},{12,16},{16,20},{20,24},{24,28},{28,0},{1,5},{5... | collective-permute-start | bytes 688136 | tf_op jit(solution)/shard_map/ppermute | solution.py:23
  25.1 6.1 %collective-permute-start.4 = (bf16[4,224,128]{2,1,0:T(8,128)(2,1)S(1)}, bf16[4,224,128]{2,1,0:T(8,128)(2,1)S(1)}, u32[]{:S(2)}, u32[]{:S(2)}) collective-permute-start(bf16[4,224,128]{2,1,0:T(8,128)(2,1)S(1)} %get-tuple-element.38), channel_id=1, source_target_pairs={{0,28},{4,0},{8,4},{12,8},{16,12},{20,16},{24,20},{28,24},{1,29},{... | collective-permute-start | bytes 688136 | tf_op jit(solution)/shard_map/ppermute | solution.py:23
  31.2 6.5 %collective-permute-start.14 = (bf16[4,224,128]{2,1,0:T(8,128)(2,1)S(1)}, bf16[4,224,128]{2,1,0:T(8,128)(2,1)S(1)}, u32[]{:S(2)}, u32[]{:S(2)}) collective-permute-start(bf16[4,224,128]{2,1,0:T(8,128)(2,1)S(1)} %get-tuple-element.54), channel_id=1, source_target_pairs={{0,4},{4,8},{8,12},{12,16},{16,20},{20,24},{24,28},{28,0},{1,5},{5... | collective-permute-start | bytes 688136 | tf_op jit(solution)/shard_map/ppermute | solution.py:23
  33.3 5.2 %collective-permute-start.15 = (bf16[4,224,128]{2,1,0:T(8,128)(2,1)S(1)}, bf16[4,224,128]{2,1,0:T(8,128)(2,1)S(1)}, u32[]{:S(2)}, u32[]{:S(2)}) collective-permute-start(bf16[4,224,128]{2,1,0:T(8,128)(2,1)S(1)} %get-tuple-element.55), channel_id=1, source_target_pairs={{0,28},{4,0},{8,4},{12,8},{16,12},{20,16},{24,20},{28,24},{1,29},{... | collective-permute-start | bytes 688136 | tf_op jit(solution)/shard_map/ppermute | solution.py:23
  34.6 6.3 %collective-permute-start.9 = (bf16[2,288,128]{2,1,0:T(8,128)(2,1)S(1)}, bf16[2,288,128]{2,1,0:T(8,128)(2,1)S(1)}, u32[]{:S(2)}, u32[]{:S(2)}) collective-permute-start(bf16[2,288,128]{2,1,0:T(8,128)(2,1)S(1)} %get-tuple-element.49), channel_id=1, source_target_pairs={{0,4},{4,8},{8,12},{12,16},{16,20},{20,24},{24,28},{28,0},{1,5},{5... | collective-permute-start | bytes 442376 | tf_op jit(solution)/shard_map/ppermute | solution.py:23
  35.4 5.5 %collective-permute-start.10 = (bf16[2,288,128]{2,1,0:T(8,128)(2,1)S(1)}, bf16[2,288,128]{2,1,0:T(8,128)(2,1)S(1)}, u32[]{:S(2)}, u32[]{:S(2)}) collective-permute-start(bf16[2,288,128]{2,1,0:T(8,128)(2,1)S(1)} %get-tuple-element.51), channel_id=1, source_target_pairs={{0,28},{4,0},{8,4},{12,8},{16,12},{20,16},{24,20},{28,24},{1,29},{... | collective-permute-start | bytes 442376 | tf_op jit(solution)/shard_map/ppermute | solution.py:23
  38.5 6.9 %collective-permute-start.16 = (bf16[2,224,128]{2,1,0:T(8,128)(2,1)S(1)}, bf16[2,224,128]{2,1,0:T(8,128)(2,1)S(1)}, u32[]{:S(2)}, u32[]{:S(2)}) collective-permute-start(bf16[2,224,128]{2,1,0:T(8,128)(2,1)S(1)} %get-tuple-element.57), channel_id=1, source_target_pairs={{0,1},{1,0},{2,3},{3,2},{4,5},{5,4},{6,7},{7,6},{8,9},{9,8},{10,11... | collective-permute-start | bytes 344072 | tf_op jit(solution)/shard_map/ppermute | solution.py:46
  41.0 8.8 %collective-permute-start.13 = (bf16[1,288,128]{2,1,0:T(8,128)(2,1)S(1)}, bf16[1,288,128]{2,1,0:T(8,128)(2,1)S(1)}, u32[]{:S(2)}, u32[]{:S(2)}) collective-permute-start(bf16[1,288,128]{2,1,0:T(8,128)(2,1)S(1)} %get-tuple-element.62), channel_id=1, source_target_pairs={{0,20},{4,24},{8,28},{12,0},{16,4},{20,8},{24,12},{28,16},{1,21},{... | collective-permute-start | bytes 221192 | tf_op jit(solution)/shard_map/ppermute | solution.py:23
  42.2 7.6 %collective-permute-start.11 = (bf16[1,288,128]{2,1,0:T(8,128)(2,1)S(1)}, bf16[1,288,128]{2,1,0:T(8,128)(2,1)S(1)}, u32[]{:S(2)}, u32[]{:S(2)}) collective-permute-start(bf16[1,288,128]{2,1,0:T(8,128)(2,1)S(1)} %get-tuple-element.63), channel_id=1, source_target_pairs={{0,28},{4,0},{8,4},{12,8},{16,12},{20,16},{24,20},{28,24},{1,29},{... | collective-permute-start | bytes 221192 | tf_op jit(solution)/shard_map/ppermute | solution.py:23
  44.6 5.3 %collective-permute-start.12 = (bf16[1,288,128]{2,1,0:T(8,128)(2,1)S(1)}, bf16[1,288,128]{2,1,0:T(8,128)(2,1)S(1)}, u32[]{:S(2)}, u32[]{:S(2)}) collective-permute-start(bf16[1,288,128]{2,1,0:T(8,128)(2,1)S(1)} %get-tuple-element.64), channel_id=1, source_target_pairs={{0,8},{4,12},{8,16},{12,20},{16,24},{20,28},{24,0},{28,4},{1,9},{5... | collective-permute-start | bytes 221192 | tf_op jit(solution)/shard_map/ppermute | solution.py:23
  45.5 4.3 %collective-permute-start.17 = (bf16[1,224,128]{2,1,0:T(8,128)(2,1)S(1)}, bf16[1,224,128]{2,1,0:T(8,128)(2,1)S(1)}, u32[]{:S(2)}, u32[]{:S(2)}) collective-permute-start(bf16[1,224,128]{2,1,0:T(8,128)(2,1)S(1)} %add_convert_fusion.3), channel_id=1, source_target_pairs={{0,3},{1,2},{2,1},{3,0},{4,7},{5,6},{6,5},{7,4},{8,11},{9,10},{10,... | collective-permute-start | bytes 172040 | tf_op jit(solution)/shard_map/ppermute | solution.py:46
  50.8 5.1 %collective-permute-start.20 = (bf16[512,128]{1,0:T(8,128)(2,1)S(1)}, bf16[512,128]{1,0:T(8,128)(2,1)S(1)}, u32[]{:S(2)}, u32[]{:S(2)}) collective-permute-start(bf16[512,128]{1,0:T(8,128)(2,1)S(1)} %get-tuple-element.59), channel_id=1, source_target_pairs={{0,192},{64,128},{128,64},{192,0},{1,193},{65,129},{129,65},{193,1... | collective-permute-start | bytes 393224 | tf_op jit(solution)/shard_map/ppermute | solution.py:46
  53.3 3.8 %collective-permute-start.19 = (bf16[512,128]{1,0:T(8,128)(2,1)S(1)}, bf16[512,128]{1,0:T(8,128)(2,1)S(1)}, u32[]{:S(2)}, u32[]{:S(2)}) collective-permute-start(bf16[512,128]{1,0:T(8,128)(2,1)S(1)} %get-tuple-element.59), channel_id=1, source_target_pairs={{0,64},{64,0},{128,192},{192,128},{1,65},{65,1},{129,193},{193,129... | collective-permute-start | bytes 393224 | tf_op jit(solution)/shard_map/ppermute | solution.py:46
  53.3 5.5 %collective-permute-start.18 = (bf16[512,128]{1,0:T(8,128)(2,1)S(1)}, bf16[512,128]{1,0:T(8,128)(2,1)S(1)}, u32[]{:S(2)}, u32[]{:S(2)}) collective-permute-start(bf16[512,128]{1,0:T(8,128)(2,1)S(1)} %get-tuple-element.59), channel_id=1, source_target_pairs={{0,128},{64,192},{128,0},{192,64},{1,129},{65,193},{129,1},{193,65... | collective-permute-start | bytes 393224 | tf_op jit(solution)/shard_map/ppermute | solution.py:46
  58.9 22.1 %collective-permute-start.21 = (f32[512,128]{1,0:T(8,128)S(1)}, f32[512,128]{1,0:T(8,128)S(1)}, u32[]{:S(2)}, u32[]{:S(2)}) collective-permute-start(f32[512,128]{1,0:T(8,128)S(1)} %add_add_fusion), channel_id=1, source_target_pairs={{0,32},{32,0},{1,33},{33,1},{2,34},{34,2},{3,35},{35,3},{4,36},{36... | collective-permute-start | bytes 786440 | tf_op jit(solution)/shard_map/ppermute | solution.py:23
  69.9 21.6 %all-to-all-start = ((bf16[128,2,128]{2,1,0:T(2,128)(2,1)}), bf16[128,2,128]{2,1,0:T(2,128)(2,1)S(1)}, u32[]{:S(2)}, u32[]{:S(2)}) async-start(bf16[128,2,128]{2,1,0:T(2,128)(2,1)} %get-tuple-element.58), calls=%async_computation | async-start | bytes 131072 | tf_op jit(solution)/shard_map/all_to_all | solution.py:194
  91.7 2.4 %collective-permute-start.22 = (bf16[2,128]{1,0:T(2,128)(2,1)S(1)}, bf16[2,128]{1,0:T(2,128)(2,1)S(1)}, u32[]{:S(2)}, u32[]{:S(2)}) collective-permute-start(bf16[2,128]{1,0:T(2,128)(2,1)S(1)} %reduce_max.18), channel_id=1, source_target_pairs={{0,32},{32,0},{1,33},{33,1},{2,34},{34,2},{3,35},{35,3},{4,36},{36... | collective-permute-start | bytes 1544 | tf_op jit(solution)/shard_map/ppermute | solution.py:23
  (3 other events, 35.4 us)

commit v3 on v2

--- a/solution.py
+++ b/solution.py
@@ -107,7 +107,7 @@
         out_shape=[pltpu.VMEM(shape, jnp.bfloat16) for shape in out],
         in_specs=[pl.BlockSpec(memory_space=pl.ANY if name == "stage" else pltpu.HBM)],
         out_specs=[VMEM] * len(out),
-        scratch_shapes=[pltpu.SemaphoreType.DMA((8,))],
+        scratch_shapes=[pltpu.SemaphoreType.DMA((12,))],
         compiler_params=SMALL,
     )(g if name == "stage" else pltpu.with_memory_space_constraint(g, pltpu.HBM))
 
@@ -124,9 +124,9 @@
     z, y = lax.axis_index("z"), lax.axis_index("y")
     row = (y + 2) % 4
     run_copies(sems, [
-        (g_ref.at[(z + 4) % 8, :, A:], far_z_ref),
-        (g_ref.at[0:4, row, :A], up_ref),
-        (g_ref.at[4:8, row, :A], down_ref),
+        *[(g_ref.at[(z + 4) % 8, i, A:], far_z_ref.at[i]) for i in range(4)],
+        *[(g_ref.at[i, row, :A], up_ref.at[i]) for i in range(4)],
+        *[(g_ref.at[4 + i, row, :A], down_ref.at[i]) for i in range(4)],
     ])
 
 
@@ -235,20 +235,18 @@
     last = send(bf(add(pb[1:2], half[1:2])), "y", 3, swap)
 
     q, m = call(
-        quantize_kernel, ((ROWS, 128), (DEVICES // 2, 2, 128)),
+        quantize_kernel, ((ROWS, 128), (DEVICES, 2, 128)),
         block, scale, pa, a_up, a_one, a_two, a_three, pb, half, last,
         scratch=[pltpu.VMEM((ROWS, 128), jnp.float32)],
     )
 
-    m = exchange(m, ("x", "z", "y"))
+    m = exchange(m, ("x", "c", "z", "y"))
 
     far, near, mirror = send(q, "x", 2, swap), send(q, "x", 1, swap), send(q, "x", 3, swap)
     chips = add(q, far) + add(near, mirror)
     accumulated = chips + send(chips, "c", 1)
     mean_grad = bf(accumulated / scale / DEVICES)
-    m, mean_grad = together(m, mean_grad)
     m = jnp.max(m, axis=0)
-    m = jnp.maximum(m, send(m, "c", 1))
     return mean_grad, jnp.max(m, axis=0)[:BLOCKS]
 
 

time: 94.7 us -> 93.3 us (0.985)
  blocking collectives: 0 us -> 22.3 us
  starting transfers between devices: 56.4 us -> 43.8 us
  waiting for transfers between devices: 31.1 us -> 20.5 us
    all_to_all x0 -> x1, blocking collectives: none -> 22.3 us  [exchange(): return lax.all_to_all(x, axes, split_axis=0, concat_axis=0, tiled=True)]
    all_to_all x1 -> x0, starting transfers between devices: 11.1 us -> none  [exchange(): return lax.all_to_all(x, axes, split_axis=0, concat_axis=0, tiled=True)]
    all_to_all x1 -> x0, waiting for transfers between devices: 9.86 us -> none  [exchange(): return lax.all_to_all(x, axes, split_axis=0, concat_axis=0, tiled=True)]
    ppermute x17 -> x16, starting transfers between devices: 38.4 us -> 36.8 us  [shift(): return lax.ppermute(x, axis, [(i, (i + by) % n) for i in range(n)])]
    ppermute x17 -> x16, waiting for transfers between devices: 14 us -> 13.1 us  [shift(): return lax.ppermute(x, axis, [(i, (i + by) % n) for i in range(n)])]
  transfers between devices with their start and end apart: 24 -> 22, of which waited for: 14 -> 12; matrix products, arithmetic and copies ran while one was open for 1% -> 1% of each run, Pallas kernels for 3% -> 3%
where the time goes in v3:
time: 93.3 us; the launch traced here: 93.2 us
  starting transfers between devices  43.8 us (47%)
  blocking collectives  22.3 us (24%)
  waiting for transfers between devices  20.5 us (22%)
  Pallas kernels  4.27 us (5%)
  other arithmetic  1.65 us (2%)
    ppermute x16, starting transfers between devices, shift(): return lax.ppermute(x, axis, [(i, (i + by) % n) for i in range(n)])  36.8 us
    all_to_all x1, blocking collectives, exchange(): return lax.all_to_all(x, axes, split_axis=0, concat_axis=0, tiled=True)  22.3 us
    ppermute x16, waiting for transfers between devices, shift(): return lax.ppermute(x, axis, [(i, (i + by) % n) for i in range(n)])  13.1 us
    ppermute x6, waiting for transfers between devices, swap(): return lax.ppermute(x, axis, [(i, i ^ by) for i in range(SIZE[axis])])  7.37 us
    ppermute x6, starting transfers between devices, swap(): return lax.ppermute(x, axis, [(i, i ^ by) for i in range(SIZE[axis])])  7.06 us
    pallas_call x2, Pallas kernels, copied(): pl.pallas_call(body, out_shape=[pltpu.VMEM(shape, jnp.bfloat16) for shape...  1.88 us
  transfers between devices with their start and end apart: 22, of which 12 were waited for; matrix products, arithmetic and copies ran while one was open for 1% of the time, Pallas kernels for 3%

profile of v3, /device:TPU:1, one launch (start us, length us, event | category | flops | bytes accessed | tf_op | source)
XLA Modules:
  0.0 93.2 jit_solution(4834957195882529759)
XLA Ops:
  0.6 1.5 %shard_map.51 = (bf16[4,224,128]{2,1,0:T(8,128)(2,1)S(1)}, bf16[4,288,128]{2,1,0:T(8,128)(2,1)S(1)}, bf16[4,288,128]{2,1,0:T(8,128)(2,1)S(1)}) custom-call(bf16[8,4,512,128]{3,2,1,0:T(8,128)(2,1)} %bitcast.2), custom_call_target="tpu_custom_call" | custom-call | tf_op jit(solution)/shard_map/pallas_call | solution.py:105
  2.1 2.2 %collective-permute-start.5 = (bf16[4,288,128]{2,1,0:T(8,128)(2,1)S(1)}, bf16[4,288,128]{2,1,0:T(8,128)(2,1)S(1)}, u32[]{:S(2)}, u32[]{:S(2)}) collective-permute-start(bf16[4,288,128]{2,1,0:T(8,128)(2,1)S(1)} %get-tuple-element.42), channel_id=1, source_target_pairs={{0,1},{1,2},{2,3},{3,0},{4,5},{5,6},{6,7},{7,4},{8,9},{9,10},{10,1... | collective-permute-start | bytes 884744 | tf_op jit(solution)/shard_map/ppermute | solution.py:23
  4.3 1.5 %collective-permute-start.6 = (bf16[4,288,128]{2,1,0:T(8,128)(2,1)S(1)}, bf16[4,288,128]{2,1,0:T(8,128)(2,1)S(1)}, u32[]{:S(2)}, u32[]{:S(2)}) collective-permute-start(bf16[4,288,128]{2,1,0:T(8,128)(2,1)S(1)} %get-tuple-element.43), channel_id=1, source_target_pairs={{0,3},{1,0},{2,1},{3,2},{4,7},{5,4},{6,5},{7,6},{8,11},{9,8},{10,9... | collective-permute-start | bytes 884744 | tf_op jit(solution)/shard_map/ppermute | solution.py:23
  5.8 1.6 %collective-permute-start = (bf16[4,224,128]{2,1,0:T(8,128)(2,1)S(1)}, bf16[4,224,128]{2,1,0:T(8,128)(2,1)S(1)}, u32[]{:S(2)}, u32[]{:S(2)}) collective-permute-start(bf16[4,224,128]{2,1,0:T(8,128)(2,1)S(1)} %get-tuple-element.30), channel_id=1, source_target_pairs={{0,4},{4,0},{8,12},{12,8},{16,20},{20,16},{24,28},{28,24},{1,5},{5... | collective-permute-start | bytes 688136 | tf_op jit(solution)/shard_map/ppermute | solution.py:46
  7.9 2.6 %collective-permute-done.5.got_up_ref = bf16[4,288,128]{2,1,0:T(8,128)(2,1)S(1)} collective-permute-done((bf16[4,288,128]{2,1,0:T(8,128)(2,1)S(1)}, bf16[4,288,128]{2,1,0:T(8,128)(2,1)S(1)}, u32[]{:S(2)}, u32[]{:S(2)}) %collective-permute-start.5) | collective-permute-done | bytes 294944 | tf_op jit(solution)/shard_map/ppermute | solution.py:23
  11.9 1.6 %collective-permute-start.7 = (bf16[8,288,128]{2,1,0:T(8,128)(2,1)S(1)}, bf16[8,288,128]{2,1,0:T(8,128)(2,1)S(1)}, u32[]{:S(2)}, u32[]{:S(2)}) collective-permute-start(bf16[8,288,128]{2,1,0:T(8,128)(2,1)S(1)} %get-tuple-element.44), channel_id=1, source_target_pairs={{0,1},{1,2},{2,3},{3,0},{4,5},{5,6},{6,7},{7,4},{8,9},{9,10},{10,1... | collective-permute-start | bytes 1769480 | tf_op jit(solution)/shard_map/ppermute | solution.py:23
  14.8 2.3 %collective-permute-start.1 = (bf16[4,224,128]{2,1,0:T(8,128)(2,1)S(1)}, bf16[4,224,128]{2,1,0:T(8,128)(2,1)S(1)}, u32[]{:S(2)}, u32[]{:S(2)}) collective-permute-start(bf16[4,224,128]{2,1,0:T(8,128)(2,1)S(1)} %get-tuple-element.31), channel_id=1, source_target_pairs={{0,4},{4,8},{8,12},{12,16},{16,20},{20,24},{24,28},{28,0},{1,5},{5... | collective-permute-start | bytes 688136 | tf_op jit(solution)/shard_map/ppermute | solution.py:23
  17.0 4.0 %collective-permute-start.2 = (bf16[4,224,128]{2,1,0:T(8,128)(2,1)S(1)}, bf16[4,224,128]{2,1,0:T(8,128)(2,1)S(1)}, u32[]{:S(2)}, u32[]{:S(2)}) collective-permute-start(bf16[4,224,128]{2,1,0:T(8,128)(2,1)S(1)} %get-tuple-element.32), channel_id=1, source_target_pairs={{0,28},{4,0},{8,4},{12,8},{16,12},{20,16},{24,20},{28,24},{1,29},{... | collective-permute-start | bytes 688136 | tf_op jit(solution)/shard_map/ppermute | solution.py:23
  21.1 3.8 %collective-permute-done.1.got_up_ref = bf16[4,224,128]{2,1,0:T(8,128)(2,1)S(1)} collective-permute-done((bf16[4,224,128]{2,1,0:T(8,128)(2,1)S(1)}, bf16[4,224,128]{2,1,0:T(8,128)(2,1)S(1)}, u32[]{:S(2)}, u32[]{:S(2)}) %collective-permute-start.1) | collective-permute-done | bytes 229408 | tf_op jit(solution)/shard_map/ppermute | solution.py:23
  25.1 2.7 %collective-permute-start.4 = (bf16[4,224,128]{2,1,0:T(8,128)(2,1)S(1)}, bf16[4,224,128]{2,1,0:T(8,128)(2,1)S(1)}, u32[]{:S(2)}, u32[]{:S(2)}) collective-permute-start(bf16[4,224,128]{2,1,0:T(8,128)(2,1)S(1)} %get-tuple-element.36), channel_id=1, source_target_pairs={{0,28},{4,0},{8,4},{12,8},{16,12},{20,16},{24,20},{28,24},{1,29},{... | collective-permute-start | bytes 688136 | tf_op jit(solution)/shard_map/ppermute | solution.py:23
  27.8 1.2 %prepare.1 = (s32[512,128]{1,0:T(8,128)S(1)}, f32[512,128]{1,0:T(8,128)S(1)}) custom-call(s32[16]{0:T(128)S(1)} %copy-done.2, f32[4,16]{1,0:T(4,128)S(1)} %copy-done.1), custom_call_target="tpu_custom_call" | custom-call | tf_op jit(solution)/shard_map/prepare/pallas_call | solution.py:79
  29.0 2.2 %collective-permute-done.3.got_up_ref = bf16[4,224,128]{2,1,0:T(8,128)(2,1)S(1)} collective-permute-done((bf16[4,224,128]{2,1,0:T(8,128)(2,1)S(1)}, bf16[4,224,128]{2,1,0:T(8,128)(2,1)S(1)}, u32[]{:S(2)}, u32[]{:S(2)}) %collective-permute-start.3) | collective-permute-done | bytes 229408 | tf_op jit(solution)/shard_map/ppermute | solution.py:23
  31.3 2.0 %collective-permute-start.14 = (bf16[4,224,128]{2,1,0:T(8,128)(2,1)S(1)}, bf16[4,224,128]{2,1,0:T(8,128)(2,1)S(1)}, u32[]{:S(2)}, u32[]{:S(2)}) collective-permute-start(bf16[4,224,128]{2,1,0:T(8,128)(2,1)S(1)} %get-tuple-element.52), channel_id=1, source_target_pairs={{0,4},{4,8},{8,12},{12,16},{16,20},{20,24},{24,28},{28,0},{1,5},{5... | collective-permute-start | bytes 688136 | tf_op jit(solution)/shard_map/ppermute | solution.py:23
  35.4 2.0 %collective-permute-start.10 = (bf16[2,288,128]{2,1,0:T(8,128)(2,1)S(1)}, bf16[2,288,128]{2,1,0:T(8,128)(2,1)S(1)}, u32[]{:S(2)}, u32[]{:S(2)}) collective-permute-start(bf16[2,288,128]{2,1,0:T(8,128)(2,1)S(1)} %get-tuple-element.49), channel_id=1, source_target_pairs={{0,28},{4,0},{8,4},{12,8},{16,12},{20,16},{24,20},{28,24},{1,29},{... | collective-permute-start | bytes 442376 | tf_op jit(solution)/shard_map/ppermute | solution.py:23
  38.9 2.1 %collective-permute-done.9.rows_ref = bf16[2,288,128]{2,1,0:T(8,128)(2,1)S(1)} collective-permute-done((bf16[2,288,128]{2,1,0:T(8,128)(2,1)S(1)}, bf16[2,288,128]{2,1,0:T(8,128)(2,1)S(1)}, u32[]{:S(2)}, u32[]{:S(2)}) %collective-permute-start.9) | collective-permute-done | bytes 147488 | tf_op jit(solution)/shard_map/ppermute | solution.py:23
  41.0 1.2 %collective-permute-start.13 = (bf16[1,288,128]{2,1,0:T(8,128)(2,1)S(1)}, bf16[1,288,128]{2,1,0:T(8,128)(2,1)S(1)}, u32[]{:S(2)}, u32[]{:S(2)}) collective-permute-start(bf16[1,288,128]{2,1,0:T(8,128)(2,1)S(1)} %get-tuple-element.58), channel_id=1, source_target_pairs={{0,20},{4,24},{8,28},{12,0},{16,4},{20,8},{24,12},{28,16},{1,21},{... | collective-permute-start | bytes 221192 | tf_op jit(solution)/shard_map/ppermute | solution.py:23
  42.3 2.4 %collective-permute-start.11 = (bf16[1,288,128]{2,1,0:T(8,128)(2,1)S(1)}, bf16[1,288,128]{2,1,0:T(8,128)(2,1)S(1)}, u32[]{:S(2)}, u32[]{:S(2)}) collective-permute-start(bf16[1,288,128]{2,1,0:T(8,128)(2,1)S(1)} %get-tuple-element.59), channel_id=1, source_target_pairs={{0,28},{4,0},{8,4},{12,8},{16,12},{20,16},{24,20},{28,24},{1,29},{... | collective-permute-start | bytes 221192 | tf_op jit(solution)/shard_map/ppermute | solution.py:23
  46.7 3.1 %collective-permute-done.17.last_ref = bf16[1,224,128]{2,1,0:T(8,128)(2,1)S(1)} collective-permute-done((bf16[1,224,128]{2,1,0:T(8,128)(2,1)S(1)}, bf16[1,224,128]{2,1,0:T(8,128)(2,1)S(1)}, u32[]{:S(2)}, u32[]{:S(2)}) %collective-permute-start.17) | collective-permute-done | bytes 57376 | tf_op jit(solution)/shard_map/ppermute | solution.py:46
  50.3 2.6 %collective-permute-start.20 = (bf16[512,128]{1,0:T(8,128)(2,1)S(1)}, bf16[512,128]{1,0:T(8,128)(2,1)S(1)}, u32[]{:S(2)}, u32[]{:S(2)}) collective-permute-start(bf16[512,128]{1,0:T(8,128)(2,1)S(1)} %get-tuple-element.56), channel_id=1, source_target_pairs={{0,192},{64,128},{128,64},{192,0},{1,193},{65,129},{129,65},{193,1... | collective-permute-start | bytes 393224 | tf_op jit(solution)/shard_map/ppermute | solution.py:46
  52.9 1.4 %collective-permute-start.18 = (bf16[512,128]{1,0:T(8,128)(2,1)S(1)}, bf16[512,128]{1,0:T(8,128)(2,1)S(1)}, u32[]{:S(2)}, u32[]{:S(2)}) collective-permute-start(bf16[512,128]{1,0:T(8,128)(2,1)S(1)} %get-tuple-element.56), channel_id=1, source_target_pairs={{0,128},{64,192},{128,0},{192,64},{1,129},{65,193},{129,1},{193,65... | collective-permute-start | bytes 393224 | tf_op jit(solution)/shard_map/ppermute | solution.py:46
  54.3 1.5 %collective-permute-done.20 = bf16[512,128]{1,0:T(8,128)(2,1)S(1)} collective-permute-done((bf16[512,128]{1,0:T(8,128)(2,1)S(1)}, bf16[512,128]{1,0:T(8,128)(2,1)S(1)}, u32[]{:S(2)}, u32[]{:S(2)}) %collective-permute-start.20) | collective-permute-done | bytes 131104 | tf_op jit(solution)/shard_map/ppermute | solution.py:46
  56.7 1.8 %collective-permute-done.18 = bf16[512,128]{1,0:T(8,128)(2,1)S(1)} collective-permute-done((bf16[512,128]{1,0:T(8,128)(2,1)S(1)}, bf16[512,128]{1,0:T(8,128)(2,1)S(1)}, u32[]{:S(2)}, u32[]{:S(2)}) %collective-permute-start.18) | collective-permute-done | bytes 131104 | tf_op jit(solution)/shard_map/ppermute | solution.py:46
  58.6 10.9 %collective-permute-start.21 = (f32[512,128]{1,0:T(8,128)S(1)}, f32[512,128]{1,0:T(8,128)S(1)}, u32[]{:S(2)}, u32[]{:S(2)}) collective-permute-start(f32[512,128]{1,0:T(8,128)S(1)} %add_add_fusion), channel_id=1, source_target_pairs={{0,32},{32,0},{1,33},{33,1},{2,34},{34,2},{3,35},{35,3},{4,36},{36... | collective-permute-start | bytes 786440 | tf_op jit(solution)/shard_map/ppermute | solution.py:23
  69.5 22.3 %all_to_all.5 = bf16[256,2,128]{2,1,0:T(2,128)(2,1)S(1)} all-to-all(bf16[256,2,128]{2,1,0:T(2,128)(2,1)S(1)} %get-tuple-element.57), channel_id=1, replica_groups=mesh['x'=4,'c'=2,'z'=8,'y'=4] {'x','c','z','y'}, dimensions={0} | all-to-all | bytes 262144 | tf_op jit(solution)/shard_map/all_to_all | solution.py:194
  (42 shorter events, 12.0 us)
Async XLA Ops:
  2.1 8.4 %collective-permute-start.5 = (bf16[4,288,128]{2,1,0:T(8,128)(2,1)S(1)}, bf16[4,288,128]{2,1,0:T(8,128)(2,1)S(1)}, u32[]{:S(2)}, u32[]{:S(2)}) collective-permute-start(bf16[4,288,128]{2,1,0:T(8,128)(2,1)S(1)} %get-tuple-element.42), channel_id=1, source_target_pairs={{0,1},{1,2},{2,3},{3,0},{4,5},{5,6},{6,7},{7,4},{8,9},{9,10},{10,1... | collective-permute-start | bytes 884744 | tf_op jit(solution)/shard_map/ppermute | solution.py:23
  4.3 7.4 %collective-permute-start.6 = (bf16[4,288,128]{2,1,0:T(8,128)(2,1)S(1)}, bf16[4,288,128]{2,1,0:T(8,128)(2,1)S(1)}, u32[]{:S(2)}, u32[]{:S(2)}) collective-permute-start(bf16[4,288,128]{2,1,0:T(8,128)(2,1)S(1)} %get-tuple-element.43), channel_id=1, source_target_pairs={{0,3},{1,0},{2,1},{3,2},{4,7},{5,4},{6,5},{7,6},{8,11},{9,8},{10,9... | collective-permute-start | bytes 884744 | tf_op jit(solution)/shard_map/ppermute | solution.py:23
  5.8 8.8 %collective-permute-start = (bf16[4,224,128]{2,1,0:T(8,128)(2,1)S(1)}, bf16[4,224,128]{2,1,0:T(8,128)(2,1)S(1)}, u32[]{:S(2)}, u32[]{:S(2)}) collective-permute-start(bf16[4,224,128]{2,1,0:T(8,128)(2,1)S(1)} %get-tuple-element.30), channel_id=1, source_target_pairs={{0,4},{4,0},{8,12},{12,8},{16,20},{20,16},{24,28},{28,24},{1,5},{5... | collective-permute-start | bytes 688136 | tf_op jit(solution)/shard_map/ppermute | solution.py:46
  11.9 22.6 %collective-permute-start.7 = (bf16[8,288,128]{2,1,0:T(8,128)(2,1)S(1)}, bf16[8,288,128]{2,1,0:T(8,128)(2,1)S(1)}, u32[]{:S(2)}, u32[]{:S(2)}) collective-permute-start(bf16[8,288,128]{2,1,0:T(8,128)(2,1)S(1)} %get-tuple-element.44), channel_id=1, source_target_pairs={{0,1},{1,2},{2,3},{3,0},{4,5},{5,6},{6,7},{7,4},{8,9},{9,10},{10,1... | collective-permute-start | bytes 1769480 | tf_op jit(solution)/shard_map/ppermute | solution.py:23
  13.5 14.3 %copy-start.1 = (f32[4,16]{1,0:T(4,128)S(1)}, f32[4,16]{1,0:T(4,128)}, u32[]{:S(2)}) copy-start(f32[4,16]{1,0:T(4,128)} %hist_ref.1) | copy-start | bytes 772
  13.5 14.3 %copy-start.2 = (s32[16]{0:T(128)S(1)}, s32[16]{0:T(128)}, u32[]{:S(2)}) copy-start(s32[16]{0:T(128)} %len_ref) | copy-start | bytes 196
  13.5 21.0 %collective-permute-start.8 = (bf16[8,288,128]{2,1,0:T(8,128)(2,1)S(1)}, bf16[8,288,128]{2,1,0:T(8,128)(2,1)S(1)}, u32[]{:S(2)}, u32[]{:S(2)}) collective-permute-start(bf16[8,288,128]{2,1,0:T(8,128)(2,1)S(1)} %get-tuple-element.45), channel_id=1, source_target_pairs={{0,3},{1,0},{2,1},{3,2},{4,7},{5,4},{6,5},{7,6},{8,11},{9,8},{10,9... | collective-permute-start | bytes 1769480 | tf_op jit(solution)/shard_map/ppermute | solution.py:23
  14.8 10.1 %collective-permute-start.1 = (bf16[4,224,128]{2,1,0:T(8,128)(2,1)S(1)}, bf16[4,224,128]{2,1,0:T(8,128)(2,1)S(1)}, u32[]{:S(2)}, u32[]{:S(2)}) collective-permute-start(bf16[4,224,128]{2,1,0:T(8,128)(2,1)S(1)} %get-tuple-element.31), channel_id=1, source_target_pairs={{0,4},{4,8},{8,12},{12,16},{16,20},{20,24},{24,28},{28,0},{1,5},{5... | collective-permute-start | bytes 688136 | tf_op jit(solution)/shard_map/ppermute | solution.py:23
  17.0 7.9 %collective-permute-start.2 = (bf16[4,224,128]{2,1,0:T(8,128)(2,1)S(1)}, bf16[4,224,128]{2,1,0:T(8,128)(2,1)S(1)}, u32[]{:S(2)}, u32[]{:S(2)}) collective-permute-start(bf16[4,224,128]{2,1,0:T(8,128)(2,1)S(1)} %get-tuple-element.32), channel_id=1, source_target_pairs={{0,28},{4,0},{8,4},{12,8},{16,12},{20,16},{24,20},{28,24},{1,29},{... | collective-permute-start | bytes 688136 | tf_op jit(solution)/shard_map/ppermute | solution.py:23
  25.0 6.2 %collective-permute-start.3 = (bf16[4,224,128]{2,1,0:T(8,128)(2,1)S(1)}, bf16[4,224,128]{2,1,0:T(8,128)(2,1)S(1)}, u32[]{:S(2)}, u32[]{:S(2)}) collective-permute-start(bf16[4,224,128]{2,1,0:T(8,128)(2,1)S(1)} %get-tuple-element.35), channel_id=1, source_target_pairs={{0,4},{4,8},{8,12},{12,16},{16,20},{20,24},{24,28},{28,0},{1,5},{5... | collective-permute-start | bytes 688136 | tf_op jit(solution)/shard_map/ppermute | solution.py:23
  25.1 6.1 %collective-permute-start.4 = (bf16[4,224,128]{2,1,0:T(8,128)(2,1)S(1)}, bf16[4,224,128]{2,1,0:T(8,128)(2,1)S(1)}, u32[]{:S(2)}, u32[]{:S(2)}) collective-permute-start(bf16[4,224,128]{2,1,0:T(8,128)(2,1)S(1)} %get-tuple-element.36), channel_id=1, source_target_pairs={{0,28},{4,0},{8,4},{12,8},{16,12},{20,16},{24,20},{28,24},{1,29},{... | collective-permute-start | bytes 688136 | tf_op jit(solution)/shard_map/ppermute | solution.py:23
  31.3 6.5 %collective-permute-start.14 = (bf16[4,224,128]{2,1,0:T(8,128)(2,1)S(1)}, bf16[4,224,128]{2,1,0:T(8,128)(2,1)S(1)}, u32[]{:S(2)}, u32[]{:S(2)}) collective-permute-start(bf16[4,224,128]{2,1,0:T(8,128)(2,1)S(1)} %get-tuple-element.52), channel_id=1, source_target_pairs={{0,4},{4,8},{8,12},{12,16},{16,20},{20,24},{24,28},{28,0},{1,5},{5... | collective-permute-start | bytes 688136 | tf_op jit(solution)/shard_map/ppermute | solution.py:23
  33.4 5.2 %collective-permute-start.15 = (bf16[4,224,128]{2,1,0:T(8,128)(2,1)S(1)}, bf16[4,224,128]{2,1,0:T(8,128)(2,1)S(1)}, u32[]{:S(2)}, u32[]{:S(2)}) collective-permute-start(bf16[4,224,128]{2,1,0:T(8,128)(2,1)S(1)} %get-tuple-element.53), channel_id=1, source_target_pairs={{0,28},{4,0},{8,4},{12,8},{16,12},{20,16},{24,20},{28,24},{1,29},{... | collective-permute-start | bytes 688136 | tf_op jit(solution)/shard_map/ppermute | solution.py:23
  34.7 6.3 %collective-permute-start.9 = (bf16[2,288,128]{2,1,0:T(8,128)(2,1)S(1)}, bf16[2,288,128]{2,1,0:T(8,128)(2,1)S(1)}, u32[]{:S(2)}, u32[]{:S(2)}) collective-permute-start(bf16[2,288,128]{2,1,0:T(8,128)(2,1)S(1)} %get-tuple-element.47), channel_id=1, source_target_pairs={{0,4},{4,8},{8,12},{12,16},{16,20},{20,24},{24,28},{28,0},{1,5},{5... | collective-permute-start | bytes 442376 | tf_op jit(solution)/shard_map/ppermute | solution.py:23
  35.4 5.5 %collective-permute-start.10 = (bf16[2,288,128]{2,1,0:T(8,128)(2,1)S(1)}, bf16[2,288,128]{2,1,0:T(8,128)(2,1)S(1)}, u32[]{:S(2)}, u32[]{:S(2)}) collective-permute-start(bf16[2,288,128]{2,1,0:T(8,128)(2,1)S(1)} %get-tuple-element.49), channel_id=1, source_target_pairs={{0,28},{4,0},{8,4},{12,8},{16,12},{20,16},{24,20},{28,24},{1,29},{... | collective-permute-start | bytes 442376 | tf_op jit(solution)/shard_map/ppermute | solution.py:23
  38.6 6.9 %collective-permute-start.16 = (bf16[2,224,128]{2,1,0:T(8,128)(2,1)S(1)}, bf16[2,224,128]{2,1,0:T(8,128)(2,1)S(1)}, u32[]{:S(2)}, u32[]{:S(2)}) collective-permute-start(bf16[2,224,128]{2,1,0:T(8,128)(2,1)S(1)} %get-tuple-element.55), channel_id=1, source_target_pairs={{0,1},{1,0},{2,3},{3,2},{4,5},{5,4},{6,7},{7,6},{8,9},{9,8},{10,11... | collective-permute-start | bytes 344072 | tf_op jit(solution)/shard_map/ppermute | solution.py:46
  41.0 8.8 %collective-permute-start.13 = (bf16[1,288,128]{2,1,0:T(8,128)(2,1)S(1)}, bf16[1,288,128]{2,1,0:T(8,128)(2,1)S(1)}, u32[]{:S(2)}, u32[]{:S(2)}) collective-permute-start(bf16[1,288,128]{2,1,0:T(8,128)(2,1)S(1)} %get-tuple-element.58), channel_id=1, source_target_pairs={{0,20},{4,24},{8,28},{12,0},{16,4},{20,8},{24,12},{28,16},{1,21},{... | collective-permute-start | bytes 221192 | tf_op jit(solution)/shard_map/ppermute | solution.py:23
  42.3 7.6 %collective-permute-start.11 = (bf16[1,288,128]{2,1,0:T(8,128)(2,1)S(1)}, bf16[1,288,128]{2,1,0:T(8,128)(2,1)S(1)}, u32[]{:S(2)}, u32[]{:S(2)}) collective-permute-start(bf16[1,288,128]{2,1,0:T(8,128)(2,1)S(1)} %get-tuple-element.59), channel_id=1, source_target_pairs={{0,28},{4,0},{8,4},{12,8},{16,12},{20,16},{24,20},{28,24},{1,29},{... | collective-permute-start | bytes 221192 | tf_op jit(solution)/shard_map/ppermute | solution.py:23
  44.7 5.3 %collective-permute-start.12 = (bf16[1,288,128]{2,1,0:T(8,128)(2,1)S(1)}, bf16[1,288,128]{2,1,0:T(8,128)(2,1)S(1)}, u32[]{:S(2)}, u32[]{:S(2)}) collective-permute-start(bf16[1,288,128]{2,1,0:T(8,128)(2,1)S(1)} %get-tuple-element.60), channel_id=1, source_target_pairs={{0,8},{4,12},{8,16},{12,20},{16,24},{20,28},{24,0},{28,4},{1,9},{5... | collective-permute-start | bytes 221192 | tf_op jit(solution)/shard_map/ppermute | solution.py:23
  45.5 4.3 %collective-permute-start.17 = (bf16[1,224,128]{2,1,0:T(8,128)(2,1)S(1)}, bf16[1,224,128]{2,1,0:T(8,128)(2,1)S(1)}, u32[]{:S(2)}, u32[]{:S(2)}) collective-permute-start(bf16[1,224,128]{2,1,0:T(8,128)(2,1)S(1)} %add_convert_fusion.3), channel_id=1, source_target_pairs={{0,3},{1,2},{2,1},{3,0},{4,7},{5,6},{6,5},{7,4},{8,11},{9,10},{10,... | collective-permute-start | bytes 172040 | tf_op jit(solution)/shard_map/ppermute | solution.py:46
  50.3 5.4 %collective-permute-start.20 = (bf16[512,128]{1,0:T(8,128)(2,1)S(1)}, bf16[512,128]{1,0:T(8,128)(2,1)S(1)}, u32[]{:S(2)}, u32[]{:S(2)}) collective-permute-start(bf16[512,128]{1,0:T(8,128)(2,1)S(1)} %get-tuple-element.56), channel_id=1, source_target_pairs={{0,192},{64,128},{128,64},{192,0},{1,193},{65,129},{129,65},{193,1... | collective-permute-start | bytes 393224 | tf_op jit(solution)/shard_map/ppermute | solution.py:46
  52.9 3.8 %collective-permute-start.19 = (bf16[512,128]{1,0:T(8,128)(2,1)S(1)}, bf16[512,128]{1,0:T(8,128)(2,1)S(1)}, u32[]{:S(2)}, u32[]{:S(2)}) collective-permute-start(bf16[512,128]{1,0:T(8,128)(2,1)S(1)} %get-tuple-element.56), channel_id=1, source_target_pairs={{0,64},{64,0},{128,192},{192,128},{1,65},{65,1},{129,193},{193,129... | collective-permute-start | bytes 393224 | tf_op jit(solution)/shard_map/ppermute | solution.py:46
  52.9 5.6 %collective-permute-start.18 = (bf16[512,128]{1,0:T(8,128)(2,1)S(1)}, bf16[512,128]{1,0:T(8,128)(2,1)S(1)}, u32[]{:S(2)}, u32[]{:S(2)}) collective-permute-start(bf16[512,128]{1,0:T(8,128)(2,1)S(1)} %get-tuple-element.56), channel_id=1, source_target_pairs={{0,128},{64,192},{128,0},{192,64},{1,129},{65,193},{129,1},{193,65... | collective-permute-start | bytes 393224 | tf_op jit(solution)/shard_map/ppermute | solution.py:46
  58.6 33.9 %collective-permute-start.21 = (f32[512,128]{1,0:T(8,128)S(1)}, f32[512,128]{1,0:T(8,128)S(1)}, u32[]{:S(2)}, u32[]{:S(2)}) collective-permute-start(f32[512,128]{1,0:T(8,128)S(1)} %add_add_fusion), channel_id=1, source_target_pairs={{0,32},{32,0},{1,33},{33,1},{2,34},{34,2},{3,35},{35,3},{4,36},{36... | collective-permute-start | bytes 786440 | tf_op jit(solution)/shard_map/ppermute | solution.py:23
  (1 other events, 6.9 us)
